TPU v7x, 8 devices: a whole 2x2x1 slice. The times are simulated.
8 devices in a mesh: dp: 1 (over z), tp: 2 (over y), sp: 4 (over x, core).
Axes of the slice: x: 2, y: 2, z: 1, core: 2. Of those that a mesh axis runs over, the one named last changes fastest.
Arguments:
- hidden: bfloat16 [128, 2880], P('dp')
- seq_lens: int32 [128], P('dp')
- rope_cos: float32 [128, 32], P('dp')
- rope_sin: float32 [128, 32], P('dp')
- k_cache: bfloat16 [128, 512, 8, 64], P('dp', 'sp', 'tp')
- v_cache: bfloat16 [128, 512, 8, 64], P('dp', 'sp', 'tp')
- norm_gain: bfloat16 [2880], replicated
- w_qkv: bfloat16 [2880, 8, 640], P(None, 'tp')
- b_qkv: bfloat16 [8, 640], P('tp')
- sink_logits: float32 [64], P('tp')
- w_o: bfloat16 [4096, 2880], P('tp')
- b_o: bfloat16 [2880], replicated
Outputs:
- output 1: bfloat16 [128, 2880], P('dp')
- output 2: bfloat16 [128, 512, 8, 64], P('dp', 'sp', 'tp')
- output 3: bfloat16 [128, 512, 8, 64], P('dp', 'sp', 'tp')
All inputs are finite; a program needn't handle non-finite values.
Results may differ from a plain program's by a relative error of at most 0.00539607.
Values sent between devices are 32-bit elements.
A program may use at most 1 GiB of HBM per device.

v0:
```python
import jax
import jax.numpy as jnp
from jax import lax
from jax.sharding import PartitionSpec as P

NORM_EPS = 1e-5


def rotate_half(heads_in, cos_part, sin_part):
    half_dim = heads_in.shape[-1] // 2
    first_half = heads_in[..., :half_dim]
    second_half = heads_in[..., half_dim:]
    return jnp.concatenate([first_half * cos_part - second_half * sin_part, second_half * cos_part + first_half * sin_part], axis=-1)


def local_partials(hidden, seq_lens, rope_cos, rope_sin, k_cache, v_cache, norm_gain, w_qkv, b_qkv, sink_logits):
    num_seqs, ctx_local, kv_local, head_dim = k_cache.shape
    group_size = w_qkv.shape[2] // head_dim - 2
    x_wide = hidden.astype(jnp.float32)
    inv_rms = lax.rsqrt(jnp.mean(x_wide * x_wide, axis=-1, keepdims=True) + NORM_EPS)
    normed = (x_wide * inv_rms * norm_gain.astype(jnp.float32)).astype(jnp.bfloat16)
    qkv_all = jnp.einsum("bd,dkc->bkc", normed, w_qkv, preferred_element_type=jnp.float32) + b_qkv.astype(jnp.float32)
    qkv_all = qkv_all.reshape(num_seqs, kv_local, group_size + 2, head_dim)
    q_rot = rotate_half(qkv_all[:, :, :group_size], rope_cos[:, None, None, :], rope_sin[:, None, None, :]).astype(jnp.bfloat16)
    k_new = rotate_half(qkv_all[:, :, group_size], rope_cos[:, None, :], rope_sin[:, None, :]).astype(jnp.bfloat16)
    v_new = qkv_all[:, :, group_size + 1].astype(jnp.bfloat16)
    positions = lax.axis_index("sp") * ctx_local + jnp.arange(ctx_local)
    is_new = (positions[None, :] == seq_lens[:, None])[:, :, None, None]
    k_out = jnp.where(is_new, k_new[:, None], k_cache)
    v_out = jnp.where(is_new, v_new[:, None], v_cache)
    logits = jnp.einsum("bkgd,blkd->bkgl", q_rot, k_out, preferred_element_type=jnp.float32) * head_dim ** -0.5
    logits = jnp.where((positions[None, :] <= seq_lens[:, None])[:, None, None, :], logits, -jnp.inf)
    row_max = jnp.maximum(jnp.max(logits, axis=-1), sink_logits.reshape(kv_local, group_size))
    weights = jnp.exp(logits - row_max[..., None])
    row_sum = jnp.sum(weights, axis=-1)
    weighted = jnp.einsum("bkgl,blkd->bkgd", weights.astype(jnp.bfloat16), v_out, preferred_element_type=jnp.float32)
    packed = jnp.concatenate([row_max[..., None], row_sum[..., None], weighted], axis=-1)
    return packed.reshape(num_seqs, kv_local * group_size, head_dim + 2), k_out, v_out


def combine_shards(parts_in, sinks_here):
    shard_max = parts_in[..., 0]
    shard_sum = parts_in[..., 1]
    top_max = jnp.max(shard_max, axis=1)
    rescale = jnp.exp(shard_max - top_max[:, None])
    denominator = jnp.sum(shard_sum * rescale, axis=1) + jnp.exp(sinks_here[None, :] - top_max)
    combined = jnp.sum(parts_in[..., 2:] * rescale[..., None], axis=1)
    return combined / denominator[..., None]


def solution(mesh):
    sp_size = mesh.shape["sp"]
    cache_spec = P("dp", "sp", "tp", None)

    def block_step(hidden, seq_lens, rope_cos, rope_sin, k_cache, v_cache, norm_gain, w_qkv, b_qkv, sink_logits, w_o, b_o):
        packed, k_out, v_out = local_partials(hidden, seq_lens, rope_cos, rope_sin, k_cache, v_cache, norm_gain, w_qkv, b_qkv, sink_logits)
        num_seqs, local_heads, width = packed.shape
        head_dim = width - 2
        head_share = local_heads // sp_size
        received = lax.all_to_all(packed.reshape(num_seqs, sp_size, head_share, width), "sp", 1, 1, tiled=True)
        sp_index = lax.axis_index("sp")
        sinks_here = sink_logits.reshape(sp_size, head_share)[sp_index]
        combined = combine_shards(received, sinks_here)
        w_rows = w_o.reshape(sp_size, head_share * head_dim, w_o.shape[1])[sp_index]
        partial_out = jnp.dot(combined.astype(jnp.bfloat16).reshape(num_seqs, head_share * head_dim), w_rows, preferred_element_type=jnp.float32)
        summed = lax.psum(partial_out, ("tp", "sp"))
        out_hidden = (hidden.astype(jnp.float32) + summed + b_o.astype(jnp.float32)).astype(jnp.bfloat16)
        return out_hidden, k_out, v_out

    return jax.shard_map(block_step, mesh=mesh, in_specs=(P("dp", None), P("dp"), P("dp", None), P("dp", None), cache_spec, cache_spec, P(None), P(None, "tp", None), P("tp", None), P("tp"), P("tp", None), P(None)), out_specs=(P("dp", None), cache_spec, cache_spec), check_vma=False)
```

profile of v0, /device:TPU:0, one launch (start us, length us, event | category | flops | bytes accessed | tf_op | source)
XLA Modules:
  0.0 148.9 jit_solution(10015408648472816947)
XLA Ops:
  7.2 0.7 convert_element_type.50
  7.9 0.7 convert_element_type.52
  8.6 1.5 %fusion.8 = f32[128]{0:T(128)S(1)} fusion(bf16[128,2880]{0,1:T(8,128)(2,1)} %param.12), kind=kLoop, calls=%fused_computation.18 | loop fusion | flops 1105792 | bytes 737792 | tf_op jit(solution)/shard_map/reduce_sum | solution.py:20
  10.1 7.8 %fusion.13 = f32[128,4,640]{2,0,1:T(8,128)S(1)} fusion(bf16[2880,4,640]{2,1,0:T(4,128)(2,1)} %param.19, bf16[128,2880]{0,1:T(8,128)(2,1)} %param.12, f32[2880]{0:T(1024)S(1)} %convert_element_type.50, f32[128]{0:T(128)S(1)} %add_rsqrt_fusion, f32[4,640]{1,0:T(4,128)S(1)} %convert_element_type.52), kind=kOutput, calls=%fused_computation.23 | convolution fusion | flops 1889239040 | bytes 16815872 | tf_op jit(solution)/shard_map/bd,dkc->bkc/dot_general | solution.py:22
  17.8 0.0 copy-start.6
  17.9 0.0 copy-start.5
  17.9 0.4 copy.59
  18.3 0.9 fusion.39
  19.2 0.1 copy.61
  19.3 0.1 copy.63
  19.4 0.1 copy.64
  19.6 0.1 copy.68
  19.7 0.0 copy-start.9
  19.7 0.0 copy-start.8
  19.8 2.9 %copy.81 = f32[128,4,8,32]{3,2,1,0:T(8,128)S(1)} copy(f32[128,4,8,32]{0,3,2,1:T(8,128)} %get-tuple-element.6) | data formatting | bytes 1048576
  22.6 2.8 %copy.82 = f32[128,4,8,32]{3,2,1,0:T(8,128)} copy(f32[128,4,8,32]{0,3,2,1:T(8,128)S(1)} %get-tuple-element.5) | data formatting | bytes 1048576
  25.5 0.1 max.22
  25.5 0.1 broadcast_compare_fusion.1
  25.6 2.2 %subtract_convert_fusion = (bf16[128,4,8,32]{3,2,1,0:T(8,128)(2,1)S(1)}, bf16[128,4,8,32]{3,2,1,0:T(8,128)(2,1)S(1)}) fusion(f32[128,4,8,32]{3,2,1,0:T(8,128)} %copy.82, f32[128,4,8,32]{3,2,1,0:T(8,128)S(1)} %copy.81, f32[128,32]{1,0:T(8,128)S(1)} %copy.63, f32[128,32]{1,0:T(8,128)S(1)} %copy.61), kind=kLoop, calls=%fused_computation.14 | loop fusion | flops 1048576 | bytes 1605632 | tf_op jit(solution)/shard_map/convert.3
  27.8 11.3 %broadcast_select_fusion.1 = (bf16[128,128,4,64]{1,3,2,0:T(8,128)(2,1)S(1)}, bf16[128,128,4,64]{1,3,2,0:T(8,128)(2,1)S(1)}) fusion(bf16[128,128,4,64]{1,3,2,0:T(8,128)(2,1)} %param.16, pred[128,128]{1,0:T(8,128)(4,1)S(1)} %get-tuple-element.12, bf16[128,4,64]{2,1,0:T(4,128)(2,1)S(1)} %copy.64, bf16[128,128,4,64]{1,3,2,0:T(8,128)(2,1)} %param.17, ...), kind=kLoop, calls=%fused_computation.3 | loop fusion | flops 8388608 | bytes 33701888 | tf_op jit(solution)/shard_map/jit(_where)/select_n | solution.py:29
  39.2 0.0 copy-start
  39.2 0.0 copy-start.2
  39.2 2.7 %fusion.5 = (f32[128,4,8]{2,1,0:T(4,128)S(1)}, f32[128,4,8,128]{3,2,1,0:T(8,128)S(1)}) fusion(pred[128,128]{1,0:T(8,128)(4,1)S(1)} %get-tuple-element.11, bf16[128,128,4,64]{1,3,2,0:T(8,128)(2,1)S(1)} %get-tuple-element.9, bf16[128,4,8,32]{3,2,1,0:T(8,128)(2,1)S(1)} %get-tuple-element.4, bf16[128,4,8,32]{3,2,1,0:T(8,128)(2,1)S(1)} %get-tuple-element.3), kind=kOutput, calls=%fused_computation.15 | convolution fusion | flops 69726208 | bytes 11042816 | tf_op jit(solution)/shard_map/bkgd,blkd->bkgl/dot_general | solution.py:31
  41.9 0.7 copy-done
  42.6 1.4 fusion.7
  44.0 1.4 copy-done.2
  45.3 5.9 %fusion.16 = f32[128,4,8,64]{3,2,1,0:T(8,128)} fusion(bf16[128,128,4,64]{1,3,2,0:T(8,128)(2,1)S(1)} %get-tuple-element.10, f32[128,4,8,128]{3,2,1,0:T(8,128)S(1)} %get-tuple-element.14, f32[128,4,8]{2,1,0:T(4,128)S(1)} %bitcast.46, pred[128,128]{1,0:T(8,128)(4,1)S(1)} %get-tuple-element.11), kind=kOutput, calls=%fused_computation.24 | convolution fusion | flops 69206016 | bytes 11567104 | tf_op jit(solution)/shard_map/bkgl,blkd->bkgd/dot_general | solution.py:36
  51.2 4.4 %copy.69 = f32[128,4,8,1]{3,2,1,0:T(8,128)} copy(f32[128,4,8,1]{2,1,0,3:T(4,128)S(1)} %bitcast.44) | data formatting | bytes 32768 | tf_op jit(solution)/shard_map/broadcast_in_dim | solution.py:37
  55.5 3.1 %copy.66 = f32[128,4,8,1]{3,2,1,0:T(8,128)S(1)} copy(f32[128,4,8,1]{2,1,0,3:T(4,128)S(1)} %bitcast.43) | data formatting | bytes 32768 | tf_op jit(solution)/shard_map/reduce_max | solution.py:33
  58.6 0.3 broadcast_maximum_fusion
  58.9 1.3 copy-done.1
  60.2 0.6 copy-done.4
  60.8 1.1 pad_maximum_fusion
  62.0 1.9 %copy.70 = f32[128,4,8,66]{0,2,3,1:T(8,128)} copy(f32[128,4,8,66]{3,2,1,0:T(8,128)S(1)} %pad_maximum_fusion) | data formatting | bytes 2162688 | tf_op jit(solution)/shard_map/concatenate | solution.py:37
  63.9 4.6 %all-to-all-start = ((f32[128,4,8,66]{0,2,3,1:T(8,128)}), f32[128,4,8,66]{0,2,3,1:T(8,128)S(1)}, u32[]{:S(2)}, u32[]{:S(2)}) async-start(f32[128,4,8,66]{0,2,3,1:T(8,128)} %copy.70), calls=%async_computation | async-start | bytes 2162688 | tf_op jit(solution)/shard_map/all_to_all | solution.py:60
  68.5 16.3 %copy.74 = bf16[2048,2880]{1,0:T(8,128)(2,1)} copy(bf16[2048,2880]{0,1:T(8,128)(2,1)} %param.22) | data formatting | bytes 23592960 | tf_op args[10]
  84.9 0.1 exponential_add_fusion
  85.0 0.1 copy.72
  85.1 0.1 fusion.18
  85.2 0.3 copy.80
  85.4 0.2 divide_convert_fusion
  85.6 0.2 copy.73
  85.8 0.0 copy-start.7
  85.9 0.0 copy-start.3
  85.9 4.1 %fusion.2 = f32[128,2880]{0,1:T(8,128)} fusion(bf16[128,512]{0,1:T(8,128)(2,1)S(1)} %bitcast.47, bf16[4,512,2880]{2,1,0:T(8,128)(2,1)} %bitcast.38, s32[]{:T(128)S(6)} %select_n.18), kind=kOutput, calls=%fused_computation.4 | convolution fusion | flops 377487360 | bytes 4620292 | tf_op jit(solution)/shard_map/dot_general | solution.py:65
  89.9 0.0 all-reduce.2.cloned.1.call-update
  90.0 49.4 %all-reduce.2.cloned.1.call-done = f32[128,2880]{0,1:T(8,128)} async-done(((f32[128,2880]{0,1:T(8,128)}), f32[128,2880]{0,1:T(8,128)}) %all-reduce.2.cloned.1.call-update) | async-done | bytes 1474576 | tf_op jit(solution)/shard_map/psum | solution.py:66
  139.4 2.7 %fusion.12 = bf16[128,2880]{0,1:T(8,128)(2,1)} fusion(f32[128,2880]{0,1:T(8,128)} %all-reduce.2.cloned.1.call-done, bf16[128,2880]{0,1:T(8,128)(2,1)S(1)} %copy-done.3, f32[2880]{0:T(1024)S(1)} %convert_element_type.57), kind=kLoop, calls=%fused_computation.22 | loop fusion | flops 1474560 | bytes 2960640 | tf_op jit(solution)/shard_map/convert_element_type | solution.py:67
  (23 shorter events, 0.1 us)
Async XLA Ops:
  17.8 1.3 copy-start.6
  17.9 1.4 copy-start.5
  19.7 5.7 %copy-start.9 = (f32[32]{0:T(128)S(1)}, f32[32]{0:T(128)}, u32[]{:S(2)}) copy-start(f32[32]{0:T(128)} %param.21) | copy-start | bytes 388
  19.7 5.8 %copy-start.8 = (s32[128]{0:T(128)S(1)}, s32[128]{0:T(128)}, u32[]{:S(2)}) copy-start(s32[128]{0:T(128)} %param.13) | copy-start | bytes 1540
  39.2 3.4 %copy-start = (bf16[128,128,4,64]{1,3,2,0:T(8,128)(2,1)}, bf16[128,128,4,64]{1,3,2,0:T(8,128)(2,1)S(1)}, u32[]{:S(2)}) copy-start(bf16[128,128,4,64]{1,3,2,0:T(8,128)(2,1)S(1)} %get-tuple-element.9) | copy-start | bytes 25165828
  39.2 6.1 %copy-start.2 = (bf16[128,128,4,64]{1,3,2,0:T(8,128)(2,1)}, bf16[128,128,4,64]{1,3,2,0:T(8,128)(2,1)S(1)}, u32[]{:S(2)}) copy-start(bf16[128,128,4,64]{1,3,2,0:T(8,128)(2,1)S(1)} %get-tuple-element.10) | copy-start | bytes 25165828
  58.6 1.6 %copy-start.1 = (f32[128,4,8,1]{3,2,1,0:T(8,128)S(1)}, f32[128,4,8,1]{3,2,1,0:T(8,128)}, u32[]{:S(2)}) copy-start(f32[128,4,8,1]{3,2,1,0:T(8,128)} %copy.69) | copy-start | bytes 49156
  58.6 2.2 %copy-start.4 = (f32[128,4,8,64]{3,2,1,0:T(8,128)S(1)}, f32[128,4,8,64]{3,2,1,0:T(8,128)}, u32[]{:S(2)}) copy-start(f32[128,4,8,64]{3,2,1,0:T(8,128)} %fusion.16) | copy-start | bytes 3145732
  63.9 21.0 %all-to-all-start = ((f32[128,4,8,66]{0,2,3,1:T(8,128)}), f32[128,4,8,66]{0,2,3,1:T(8,128)S(1)}, u32[]{:S(2)}, u32[]{:S(2)}) async-start(f32[128,4,8,66]{0,2,3,1:T(8,128)} %copy.70), calls=%async_computation | async-start | bytes 2162688 | tf_op jit(solution)/shard_map/all_to_all | solution.py:60
  68.5 70.9 %all-reduce.2.cloned.1.call-start = ((), (), s32[]{:S(2)}) async-start(), calls=%async_computation.1 | async-start | bytes 2949120 | tf_op jit(solution)/shard_map/psum | solution.py:66
  85.8 4.1 %copy-start.7 = (bf16[2880]{0:T(1024)(128)(2,1)S(1)}, bf16[2880]{0:T(1024)(128)(2,1)}, u32[]{:S(2)}) copy-start(bf16[2880]{0:T(1024)(128)(2,1)} %param.23) | copy-start | bytes 17284
  85.9 53.5 %copy-start.3 = (bf16[128,2880]{0,1:T(8,128)(2,1)S(1)}, bf16[128,2880]{0,1:T(8,128)(2,1)}, u32[]{:S(2)}) copy-start(bf16[128,2880]{0,1:T(8,128)(2,1)} %param.12) | copy-start | bytes 2211844
Sparse Core Ops, SparseCore 0:
  90.1 49.2 all-reduce.1
where the time goes:
time: 150 us; the launch traced here: 149 us
  waiting for transfers between devices  49.4 us (33%)
  local copies, waits for them, and re-layouts  37.8 us (25%)
  other arithmetic  22.5 us (15%)
  matrix products  20.4 us (14%)
  between operations  14.3 us (10%)
  starting transfers between devices  4.61 us (3%)
    psum x1, waiting for transfers between devices, block_step(): summed = lax.psum(partial_out, ('tp', 'sp'))  49.4 us
    unnamed x27, local copies, waits for them, and re-layouts  26.5 us
    select_n x1, other arithmetic, local_partials(): k_out = jnp.where(is_new, k_new[:, None], k_cache)  11.3 us
    dot_general x1, matrix products, local_partials(): jnp.einsum('bd,dkc->bkc', normed, w_qkv, preferred_element_type=jnp.float32)  7.76 us
    dot_general x1, matrix products, local_partials(): jnp.einsum('bkgl,blkd->bkgd', weights.astype(jnp.bfloat16), v_out, prefer...  5.85 us
    all_to_all x1, starting transfers between devices, block_step(): lax.all_to_all(packed.reshape(num_seqs, sp_size, head_share, width), 'sp'...  4.61 us
    broadcast_in_dim x1, local copies, waits for them, and re-layouts, local_partials(): row_sum[..., None]  4.37 us
    dot_general x1, matrix products, block_step(): jnp.dot(combined.astype(jnp.bfloat16).reshape(num_seqs, head_share * head...  4.08 us
  transfers between devices with their start and end apart: 2, of which 1 were waited for; matrix products, arithmetic and copies ran while one was open for 11% of the time, Pallas kernels for 0%

commit v1 on v0

v1 whole, which is shorter than its diff:
```python
import functools
import jax
import jax.numpy as jnp
from jax import lax
from jax.sharding import PartitionSpec as P
from jax.experimental import pallas as pl
from jax.experimental.pallas import tpu as pltpu

NORM_EPS = 1e-5
CHUNK = 8
GROUP = 32
ROWS = 512
MESH = pl.DeviceIdType.MESH


def attend_kernel(lens_hbm, sinks_hbm, x_hbm, gain_hbm, w_hbm, b_hbm, cos_hbm, sin_hbm, k_hbm, v_hbm,
                  k_out, v_out, part,
                  lens, sinks, x_t, gain, b_qkv, cos_t, sin_t,
                  w_buf, w_f32, acc, h_buf, q_buf, kn_t, vn_t, k_buf, v_buf, e_buf,
                  small_sem, w_sem, in_sem, out_sem):
    d_model, seqs = x_t.shape
    n_chunks = seqs // CHUNK
    n_full, tail = divmod(d_model, ROWS)

    smalls = [pltpu.make_async_copy(src, dst, small_sem.at[i]) for i, (src, dst) in enumerate(
        [(x_hbm, x_t), (gain_hbm, gain), (b_hbm, b_qkv), (cos_hbm, cos_t), (sin_hbm, sin_t), (lens_hbm, lens), (sinks_hbm, sinks)])]
    for c in smalls:
        c.start()

    def w_copies(i, n):
        rows = pl.ds(i * ROWS, n)
        return [pltpu.make_async_copy(w_hbm.at[rows, :, pl.ds(c * 128, 128)], w_buf.at[c, rows], w_sem.at[i, c]) for c in range(5)]

    for i in range(n_full):
        for c in w_copies(i, ROWS):
            c.start()
    for c in w_copies(n_full, tail):
        c.start()

    def cache_in(a, i):
        rows = pl.ds(i * CHUNK, CHUNK)
        src, dst = ((k_hbm, k_buf), (v_hbm, v_buf))[a]
        return pltpu.make_async_copy(src.at[rows], dst.at[rows], in_sem.at[a, i])

    def cache_out(a, i):
        rows = pl.ds(i * CHUNK, CHUNK)
        src, dst = ((k_buf, k_out), (v_buf, v_out))[a]
        return pltpu.make_async_copy(src.at[rows], dst.at[rows], out_sem.at[a, i])

    for c in smalls:
        c.wait()

    sq = jnp.zeros((seqs, 1), jnp.float32)
    xs = []
    for j in range(0, d_model, 128):
        n = min(128, d_model - j)
        xb = x_t[j:j + n, :].astype(jnp.float32).T
        xs.append(xb)
        sq = sq + jnp.sum(xb * xb, axis=1, keepdims=True)
    inv = lax.rsqrt(sq * (1.0 / d_model) + NORM_EPS)
    for i, j in enumerate(range(0, d_model, 128)):
        n = min(128, d_model - j)
        h_buf[:, j:j + n] = (xs[i] * inv * gain[0:1, j:j + n]).astype(jnp.bfloat16)

    bias = b_qkv[...].astype(jnp.float32)
    for p in range(2):
        for c in range(5):
            for u in range(2):
                acc[p, c, :, u * 128:u * 128 + 128] = jnp.broadcast_to(bias[2 * p + u:2 * p + u + 1, c * 128:c * 128 + 128], (seqs, 128))

    def project(i, n):
        rows = pl.multiple_of(i * ROWS, ROWS)
        h = h_buf[:, pl.ds(rows, n)]
        for c, copy in enumerate(w_copies(i, n)):
            copy.wait()
        for c in range(5):
            w_f32[c, 0:4 * n, :] = w_buf[c, pl.ds(rows, n)].reshape(4 * n, 128).astype(jnp.float32)
            for p in range(2):
                w = jnp.concatenate([w_f32[c, pl.ds(2 * p + u, n, stride=4), :].astype(jnp.bfloat16) for u in range(2)], axis=1)
                acc[p, c] += jnp.dot(h, w, preferred_element_type=jnp.float32)

    def project_step(i, carry):
        project(i, ROWS)

        @pl.when(i == 2)
        def _():
            for ch in range(n_chunks):
                cache_in(0, ch).start()

        @pl.when(i == 4)
        def _():
            for ch in range(n_chunks):
                cache_in(1, ch).start()
        return carry

    lax.fori_loop(0, n_full, project_step, 0)
    project(n_full, tail)

    lane = lax.broadcasted_iota(jnp.int32, (seqs, 128), 1)
    low = lane < 64
    first_half = (lane & 63) < 32
    cos4 = jnp.concatenate([cos_t[...]] * 4, axis=0).T
    sin4 = jnp.concatenate([sin_t[...]] * 4, axis=0).T
    sin4 = jnp.where(first_half, -sin4, sin4)

    def rotate(t):
        other = jnp.where(first_half, pltpu.roll(t, 96, 1), pltpu.roll(t, 32, 1))
        return t * cos4 + other * sin4

    for p in range(2):
        lanes = slice(p * 128, p * 128 + 128)
        for tile in range(5):
            t0 = acc[p, tile, :, 0:128]
            t1 = acc[p, tile, :, 128:256]
            even = jnp.where(low, t0, pltpu.roll(t1, 64, 1))
            odd = jnp.where(low, pltpu.roll(t0, 64, 1), t1)
            if tile < 4:
                q_buf[p, pl.ds(2 * tile, seqs, stride=8), :] = rotate(even)
                q_buf[p, pl.ds(2 * tile + 1, seqs, stride=8), :] = rotate(odd)
            else:
                kn_t[lanes, :] = rotate(even).T
                vn_t[lanes, :] = odd.T

    base = lax.axis_index("sp") * 128
    lane8 = lax.broadcasted_iota(jnp.int32, (8, 128), 1)
    row8 = lax.broadcasted_iota(jnp.int32, (8, 128), 0)
    sink_rows = []
    for k in range(4):
        t = jnp.zeros((8, 128), jnp.float32)
        for g in range(8):
            t = jnp.where(row8 == g, sinks[k * 8 + g], t)
        sink_rows.append(t)
    sink_col = jnp.concatenate(sink_rows, axis=0)[:, 0:1]
    lane32 = lax.broadcasted_iota(jnp.int32, (32, 128), 1)
    lane256 = lax.broadcasted_iota(jnp.int32, (256, 128), 1)
    q_lane = lax.broadcasted_iota(jnp.int32, (8, 256), 1) // 64
    half8 = lane8 < 64

    def put_new(buf, new_t, i):
        for u in range(CHUNK):
            b = i * CHUNK + u
            loc = lens[b] - base

            @pl.when((loc >= 0) & (loc < 128))
            def _():
                shift = lax.rem(loc - b + 256, 128)
                buf[b] = jnp.where(lane256 == loc, pltpu.roll(new_t[...], shift, 1), buf[b].astype(jnp.float32)).astype(jnp.bfloat16)

    def score_step(i, carry):
        cache_in(0, i).wait()
        put_new(k_buf, kn_t, i)
        cache_out(0, i).start()
        group = i // (GROUP // CHUNK)
        m_acc = part[group, 256:264, 0:128]
        s_acc = part[group, 256:264, 128:256]
        for u in range(CHUNK):
            b = i * CHUNK + u
            j = lax.rem(i, GROUP // CHUNK) * CHUNK + u
            rows = jnp.concatenate([q_buf[p, pl.ds(pl.multiple_of(b * 8, 8), 8), :] for p in range(2)], axis=1)
            q_blk = jnp.concatenate([jnp.where(q_lane == k, rows, 0.0) for k in range(4)], axis=0).astype(jnp.bfloat16)
            logits = jnp.dot(q_blk, k_buf[b], preferred_element_type=jnp.float32) * 0.125
            logits = jnp.where(lane32 <= lens[b] - base, logits, -jnp.inf)
            m = jnp.maximum(jnp.max(logits, axis=1, keepdims=True), sink_col)
            e = jnp.exp(logits - m)
            s = jnp.sum(e, axis=1, keepdims=True)
            e_buf[pl.ds(pl.multiple_of(b * 32, 32), 32), :] = e.astype(jnp.bfloat16)
            for k in range(4):
                here = lane8 == j * 4 + k
                m_acc = jnp.where(here, m[8 * k:8 * k + 8], m_acc)
                s_acc = jnp.where(here, s[8 * k:8 * k + 8], s_acc)
        part[group, 256:264, 0:128] = m_acc
        part[group, 256:264, 128:256] = s_acc
        return carry

    lax.fori_loop(0, n_chunks, score_step, 0)

    def value_step(i, carry):
        cache_in(1, i).wait()
        put_new(v_buf, vn_t, i)
        cache_out(1, i).start()
        group = i // (GROUP // CHUNK)
        for u in range(CHUNK):
            b = i * CHUNK + u
            j = lax.rem(i, GROUP // CHUNK) * CHUNK + u
            e = e_buf[pl.ds(pl.multiple_of(b * 32, 32), 32), :]
            r = lax.dot_general(e, v_buf[b], (((1,), (1,)), ((), ())), preferred_element_type=jnp.float32)
            rows = pl.ds(pl.multiple_of(j * 8, 8), 8)
            part[group, rows, 0:128] = jnp.where(half8, r[0:8, 0:128], r[8:16, 0:128])
            part[group, rows, 128:256] = jnp.where(half8, r[16:24, 128:256], r[24:32, 128:256])
        return carry

    lax.fori_loop(0, n_chunks, value_step, 0)

    def drain(i, carry):
        cache_out(0, i).wait()
        cache_out(1, i).wait()
        return carry

    lax.fori_loop(0, n_chunks, drain, 0)


def local_attention(hidden, seq_lens, rope_cos, rope_sin, k_cache, v_cache, norm_gain, w_qkv, b_qkv, sink_logits):
    seqs, d_model = hidden.shape
    ctx, kv, dim = k_cache.shape[1:]
    k_t = k_cache.transpose(0, 2, 3, 1).reshape(seqs, kv * dim, ctx)
    v_t = v_cache.transpose(0, 2, 3, 1).reshape(seqs, kv * dim, ctx)
    hbm = lambda a: pltpu.with_memory_space_constraint(a, pltpu.HBM)
    vmem = pl.BlockSpec(memory_space=pltpu.VMEM)
    anyw = pl.BlockSpec(memory_space=pltpu.HBM)
    n_chunks = seqs // CHUNK
    k_out, v_out, part = pl.pallas_call(
        attend_kernel,
        out_shape=(jax.ShapeDtypeStruct(k_t.shape, k_t.dtype), jax.ShapeDtypeStruct(v_t.shape, v_t.dtype),
                   jax.ShapeDtypeStruct((seqs // GROUP, GROUP * 8 + 8, kv * dim), jnp.float32)),
        in_specs=[anyw] * 10,
        out_specs=(anyw, anyw, vmem),
        scratch_shapes=[
            pltpu.SMEM((seqs,), jnp.int32),
            pltpu.SMEM((kv * 8,), jnp.float32),
            pltpu.VMEM((d_model, seqs), jnp.bfloat16),
            pltpu.VMEM((1, d_model), jnp.float32),
            pltpu.VMEM(b_qkv.shape, jnp.bfloat16),
            pltpu.VMEM((dim // 2, seqs), jnp.float32),
            pltpu.VMEM((dim // 2, seqs), jnp.float32),
            pltpu.VMEM((5, d_model, kv, 128), jnp.bfloat16),
            pltpu.VMEM((5, ROWS * kv, 128), jnp.float32),
            pltpu.VMEM((2, 5, seqs, 256), jnp.float32),
            pltpu.VMEM((seqs, 2944), jnp.bfloat16),
            pltpu.VMEM((2, seqs * 8, 128), jnp.float32),
            pltpu.VMEM((kv * dim, seqs), jnp.float32),
            pltpu.VMEM((kv * dim, seqs), jnp.float32),
            pltpu.VMEM(k_t.shape, jnp.bfloat16),
            pltpu.VMEM(v_t.shape, jnp.bfloat16),
            pltpu.VMEM((seqs * 32, 128), jnp.bfloat16),
            pltpu.SemaphoreType.DMA((7,)),
            pltpu.SemaphoreType.DMA((6, 5)),
            pltpu.SemaphoreType.DMA((2, n_chunks)),
            pltpu.SemaphoreType.DMA((2, n_chunks)),
        ],
        compiler_params=pltpu.CompilerParams(vmem_limit_bytes=56 * 1024 * 1024),
        cost_estimate=pl.CostEstimate(flops=3 * 10**9, bytes_accessed=48 * 10**6, transcendentals=10**6),
    )(hbm(seq_lens), hbm(sink_logits), hbm(hidden.T), norm_gain.astype(jnp.float32)[None, :], hbm(w_qkv), hbm(b_qkv),
      hbm(rope_cos.T), hbm(rope_sin.T), hbm(k_t), hbm(v_t))
    back = lambda a: a.reshape(seqs, kv, dim, ctx).transpose(0, 3, 1, 2)
    return back(k_out), back(v_out), part


COLS = 512
HALF = 3 * COLS


def exchange_kernel(part, sinks_hbm, bias, w_hbm, y_out,
                    sinks, w_buf, from_core, to_chip, own, from_chip, o_buf, lhs, y_buf, from_tp, gather,
                    small_sem, w_sem, core_send, core_recv, chip_send, chip_recv, tp_send, tp_recv, ag_send, ag_recv):
    tp = lax.axis_index("tp")
    sp = lax.axis_index("sp")
    core = lax.rem(sp, 2)
    chip = sp // 2
    d_out = w_hbm.shape[0]
    n_cols = [(n, min(COLS, d_out - n)) for n in range(0, d_out, COLS)]
    sibling = {"sp": sp + 1 - 2 * core}
    across_x = {"sp": lax.rem(sp + 2, 4)}
    across_y = {"tp": 1 - tp}

    small = pltpu.make_async_copy(sinks_hbm, sinks, small_sem)
    small.start()
    w_copies = [pltpu.make_async_copy(w_hbm.at[pl.ds(n, w)], w_buf.at[pl.ds(n, w)], w_sem.at[i]) for i, (n, w) in enumerate(n_cols)]
    for c in w_copies:
        c.start()

    barrier = pltpu.get_barrier_semaphore()
    for peer in (sibling, across_x, across_y):
        pl.semaphore_signal(barrier, inc=1, device_id=peer, device_id_type=MESH)
    pl.semaphore_wait(barrier, 3)

    def remote(src, dst, ss, rs, peer):
        return pltpu.make_async_remote_copy(src_ref=src, dst_ref=dst, send_sem=ss, recv_sem=rs, device_id=peer, device_id_type=MESH)

    core_copies = []
    for r in range(2):
        x_side = (1 - chip) if r == 0 else chip
        group = 2 * x_side + (1 - core)
        core_copies.append(remote(part.at[group], from_core.at[r], core_send.at[r], core_recv.at[r], sibling))
    for c in core_copies:
        c.start()

    lane = lax.broadcasted_iota(jnp.int32, (8, 128), 1)
    row = lax.broadcasted_iota(jnp.int32, (8, 128), 0)
    high = lane // 64

    def spread(f, j, p):
        return jnp.take_along_axis(f, j * 4 + 2 * p + high, axis=1)

    def stats(a, b):
        m_a, s_a = a[0], a[1]
        m_b, s_b = b[0], b[1]
        m = jnp.maximum(m_a, m_b)
        f_a = jnp.exp(m_a - m)
        f_b = jnp.exp(m_b - m)
        return m, s_a * f_a + s_b * f_b, f_a, f_b

    def stat_rows(ref):
        return ref[256:264, 0:128], ref[256:264, 128:256]

    def merge(a_ref, b_ref, out_ref, f_a, f_b, j0, j1):
        for j in range(j0, j1):
            rows = slice(8 * j, 8 * j + 8)
            for p in range(2):
                cols = slice(128 * p, 128 * p + 128)
                out_ref[rows, cols] = a_ref[rows, cols] * spread(f_a, j, p) + b_ref[rows, cols] * spread(f_b, j, p)

    pieces = [(0, 8), (8, 16), (16, 24), (24, 32)]

    def piece_rows(i):
        j0, j1 = pieces[i]
        return pl.ds(8 * j0, 8 * (j1 - j0) + (8 if i == len(pieces) - 1 else 0))

    core_copies[0].wait_recv()
    away = part.at[2 * (1 - chip) + core]
    m, s, f_a, f_b = stats(stat_rows(away), stat_rows(from_core.at[0]))
    to_chip[256:264, 0:128] = m
    to_chip[256:264, 128:256] = s
    chip_copies = [remote(to_chip.at[piece_rows(i)], from_chip.at[piece_rows(i)], chip_send.at[i], chip_recv.at[i], across_x) for i in range(len(pieces))]
    order = [3, 0, 1, 2]
    for i in order:
        merge(away, from_core.at[0], to_chip, f_a, f_b, *pieces[i])
        chip_copies[i].start()

    core_copies[1].wait_recv()
    here = part.at[2 * chip + core]
    m_own, s_own, f_a, f_b = stats(stat_rows(here), stat_rows(from_core.at[1]))
    merge(here, from_core.at[1], own, f_a, f_b, 0, 32)

    small.wait()
    sink = jnp.zeros((8, 128), jnp.float32)
    k_of_lane = lane & 3
    for k in range(4):
        for g in range(8):
            sink = jnp.where((row == g) & (k_of_lane == k), sinks[k * 8 + g], sink)

    chip_copies[3].wait_recv()
    m, s, f_a, f_b = stats((m_own, s_own), stat_rows(from_chip))
    scale = 1.0 / (s + jnp.exp(sink - m))
    f_a = f_a * scale
    f_b = f_b * scale
    for i in order:
        if i != 3:
            chip_copies[i].wait_recv()
        for j in range(*pieces[i]):
            rows = slice(8 * j, 8 * j + 8)
            for p in range(2):
                cols = slice(128 * p, 128 * p + 128)
                o_buf[p, rows, :] = own[rows, cols] * spread(f_a, j, p) + from_chip[rows, cols] * spread(f_b, j, p)

    low = lax.broadcasted_iota(jnp.int32, (32, 128), 1) < 64
    for p in range(2):
        for t in range(4):
            a = o_buf[p, pl.ds(2 * t, 32, stride=8), :]
            b = o_buf[p, pl.ds(2 * t + 1, 32, stride=8), :]
            even_k = (2 * p) * 512 + t * 128
            odd_k = (2 * p + 1) * 512 + t * 128
            lhs[:, even_k:even_k + 128] = jnp.where(low, a, pltpu.roll(b, 64, 1)).astype(jnp.bfloat16)
            lhs[:, odd_k:odd_k + 128] = jnp.where(low, pltpu.roll(a, 64, 1), b).astype(jnp.bfloat16)

    theirs = pl.ds(pl.multiple_of((1 - tp) * 16, 16), 16)
    mine = pl.ds(pl.multiple_of(tp * 16, 16), 16)
    tp_copies = []
    for i, (n, w) in enumerate(n_cols):
        w_copies[i].wait()
        y_buf[i, :, 0:w] = lax.dot_general(lhs[...], w_buf[n:n + w, :], (((1,), (1,)), ((), ())), preferred_element_type=jnp.float32)
        c = remote(y_buf.at[i, theirs], from_tp.at[i], tp_send.at[i], tp_recv.at[i], across_y)
        c.start()
        tp_copies.append(c)

    def rows_of(t, q):
        return pl.ds(pl.multiple_of(q * 32 + t * 16, 16), 16)

    def piece(t, q, half):
        cols = pl.ds(0, HALF) if half == 0 else pl.ds(HALF, gather.shape[1] - HALF)
        return gather.at[rows_of(t, q), cols]

    other_sp = lax.rem(sp + 2, 4)
    started = []

    def send(t, q, half, slot, peer):
        ref = piece(t, q, half)
        c = remote(ref, ref, ag_send.at[slot, half], ag_recv.at[slot, half], peer)
        c.start()
        started.append(c)

    def arrived(t, q, half, slot):
        ref = piece(t, q, half)
        remote(ref, ref, ag_send.at[slot, half], ag_recv.at[slot, half], sibling).wait_recv()

    for half in range(2):
        for i in range(3 * half, 3 * half + 3):
            n, w = n_cols[i]
            tp_copies[i].wait_recv()
            gather[rows_of(tp, sp), n:n + w] = y_buf[i, mine, 0:w] + from_tp[i, :, 0:w] + bias[0:1, n:n + w]
        send(tp, sp, half, 0, across_x)
        send(tp, sp, half, 1, across_y)
        send(tp, sp, half, 3, sibling)
    for half in range(2):
        arrived(tp, other_sp, half, 0)
        if half == 0:
            send(tp, other_sp, half, 2, across_y)
        send(tp, other_sp, half, 4, sibling)
        arrived(1 - tp, sp, half, 1)
        if half == 1:
            send(1 - tp, sp, half, 2, across_x)
        send(1 - tp, sp, half, 5, sibling)
    for half in range(2):
        arrived(1 - tp, other_sp, half, 2)
        send(1 - tp, other_sp, half, 6, sibling)
    sib = sp + 1 - 2 * core
    other_sib = lax.rem(sib + 2, 4)
    for half in range(2):
        arrived(tp, sib, half, 3)
        arrived(tp, other_sib, half, 4)
        arrived(1 - tp, sib, half, 5)
        arrived(1 - tp, other_sib, half, 6)
        lo, hi = (0, HALF) if half == 0 else (HALF, d_out)
        for n in range(lo, hi, 128):
            w = min(128, hi - n)
            y_out[n:n + w, :] = gather[:, n:n + w].T
    for c in core_copies + chip_copies + tp_copies + started:
        c.wait_send()


def exchange(part, sink_logits, w_o, b_o):
    d_out = w_o.shape[1]
    heads = w_o.shape[0]
    n_col = -(-d_out // COLS)
    padded = -(-d_out // 128) * 128
    hbm = lambda a: pltpu.with_memory_space_constraint(a, pltpu.HBM)
    vmem = pl.BlockSpec(memory_space=pltpu.VMEM)
    anyw = pl.BlockSpec(memory_space=pltpu.HBM)
    block = part.shape[1:]
    dma = pltpu.SemaphoreType.DMA
    return pl.pallas_call(
        exchange_kernel,
        out_shape=jax.ShapeDtypeStruct((d_out, 128), jnp.float32),
        in_specs=[vmem, anyw, vmem, anyw],
        out_specs=vmem,
        scratch_shapes=[
            pltpu.SMEM(sink_logits.shape, jnp.float32),
            pltpu.VMEM((d_out, heads), jnp.bfloat16),
            pltpu.VMEM((2,) + block, jnp.float32),
            pltpu.VMEM(block, jnp.float32),
            pltpu.VMEM(block, jnp.float32),
            pltpu.VMEM(block, jnp.float32),
            pltpu.VMEM((2, 256, 128), jnp.float32),
            pltpu.VMEM((32, heads), jnp.bfloat16),
            pltpu.VMEM((n_col, 32, COLS), jnp.float32),
            pltpu.VMEM((n_col, 16, COLS), jnp.float32),
            pltpu.VMEM((128, padded), jnp.float32),
            dma, dma((n_col,)), dma((2,)), dma((2,)), dma((4,)), dma((4,)), dma((n_col,)), dma((n_col,)), dma((7, 2)), dma((7, 2)),
        ],
        compiler_params=pltpu.CompilerParams(collective_id=0, has_side_effects=True, vmem_limit_bytes=32 * 1024 * 1024),
        cost_estimate=pl.CostEstimate(flops=4 * 10**8, bytes_accessed=16 * 10**6, transcendentals=10**5),
    )(part, hbm(sink_logits), b_o.astype(jnp.float32)[None, :], hbm(w_o.T))


def solution(mesh):
    cache_spec = P("dp", "sp", "tp", None)

    def block_step(hidden, seq_lens, rope_cos, rope_sin, k_cache, v_cache, norm_gain, w_qkv, b_qkv, sink_logits, w_o, b_o):
        k_out, v_out, part = local_attention(hidden, seq_lens, rope_cos, rope_sin, k_cache, v_cache, norm_gain, w_qkv, b_qkv, sink_logits)
        y_t = exchange(part, sink_logits, w_o, b_o)
        out_hidden = (hidden.T.astype(jnp.float32) + y_t).astype(jnp.bfloat16).T
        return out_hidden, k_out, v_out

    return jax.shard_map(block_step, mesh=mesh, in_specs=(P("dp", None), P("dp"), P("dp", None), P("dp", None), cache_spec, cache_spec, P(None), P(None, "tp", None), P("tp", None), P("tp"), P("tp", None), P(None)), out_specs=(P("dp", None), cache_spec, cache_spec), check_vma=False)
```

time: 150 us -> 71.5 us (0.48)
  Pallas kernels: 0 us -> 65.7 us
  waiting for transfers between devices: 49.4 us -> 0 us
  local copies, waits for them, and re-layouts: 37.8 us -> 3.23 us
  other arithmetic: 22.5 us -> 1.01 us
  matrix products: 20.4 us -> 0 us
  between operations: 14.3 us -> 0.67 us
  starting transfers between devices: 4.61 us -> 0 us
    pallas_call x0 -> x2, Pallas kernels: none -> 65.7 us  [the longest x1 35.3 us: local_attention(): pl.pallas_call(attend_kernel, out_shape=(jax.ShapeDtypeStruct(k_t.shape,...]
    psum x1 -> x0, waiting for transfers between devices: 49.4 us -> none  [block_step(): summed = lax.psum(partial_out, ('tp', 'sp'))]
    unnamed x27 -> x4, local copies, waits for them, and re-layouts: 26.5 us -> 1.23 us
    dot_general x4 -> x0, matrix products: 20.4 us -> none  [the longest x1 7.76 us: local_partials(): jnp.einsum('bd,dkc->bkc', normed, w_qkv, preferred_element_type=jnp.float32)]
    select_n x1 -> x0, other arithmetic: 11.3 us -> none  [local_partials(): k_out = jnp.where(is_new, k_new[:, None], k_cache)]
    all_to_all x1 -> x0, starting transfers between devices: 4.61 us -> none  [block_step(): lax.all_to_all(packed.reshape(num_seqs, sp_size, head_share, width), 'sp'...]
    convert_element_type x5 -> x0, other arithmetic: 4.28 us -> none  [the longest x1 2.68 us: block_step(): (hidden.astype(jnp.float32) + summed + b_o.astype(jnp.float32)).astype(jn...]
    reduce_max x1 -> x0, local copies, waits for them, and re-layouts: 3.07 us -> none  [local_partials(): jnp.max(logits, axis=-1)]
  transfers between devices with their start and end apart: 2 -> 0, of which waited for: 1 -> 0; matrix products, arithmetic and copies ran while one was open for 11% -> 0% of each run, Pallas kernels for 0% -> 0%
where the time goes in v1:
time: 71.5 us; the launch traced here: 70.6 us
  Pallas kernels  65.7 us (92%)
  local copies, waits for them, and re-layouts  3.23 us (5%)
  other arithmetic  1.01 us (1%)
    pallas_call x1, Pallas kernels, local_attention(): pl.pallas_call(attend_kernel, out_shape=(jax.ShapeDtypeStruct(k_t.shape,...  35.3 us
    pallas_call x1, Pallas kernels, exchange(): pl.pallas_call(exchange_kernel, out_shape=jax.ShapeDtypeStruct((d_out, 12...  30.4 us

profile of v1, /device:TPU:0, one launch (start us, length us, event | category | flops | bytes accessed | tf_op | source)
XLA Modules:
  0.0 70.6 jit_solution(7344163149905261342)
XLA Ops:
  0.6 1.3 %reshape.22.gain_hbm = f32[1,2880]{1,0:T(1,128)} reshape(bf16[2880]{0:T(1024)(128)(2,1)} %param.18) | data formatting | bytes 17280 | tf_op jit(solution)/shard_map/broadcast_in_dim | solution.py:242
  1.9 0.7 reshape.23.bias
  2.6 0.0 copy-start.1
  2.6 35.3 %shard_map.139 = (bf16[128,256,128]{2,1,0:T(8,128)(2,1)}, bf16[128,256,128]{2,1,0:T(8,128)(2,1)}, f32[4,264,256]{2,1,0:T(8,128)}) custom-call(s32[128]{0:T(128)} %lens_hbm.1, f32[32]{0:T(128)} %sinks_hbm.3, bf16[2880,128]{1,0:T(8,128)(2,1)} %bitcast.22, f32[1,2880]{1,0:T(1,128)} %reshape.22.gain_hbm, bf16[2880,4,640]{2,1,0:T(4,128)(2,1)} %w_hbm.1, ...), custom_call_target="tpu_custom_call" | custom-call | flops 3000000000 | bytes 48000000 | tf_op jit(solution)/shard_map/pallas_call | solution.py:211
  37.9 0.0 copy-start
  38.0 1.2 %copy-done = f32[4,264,256]{2,1,0:T(8,128)S(1)} copy-done((f32[4,264,256]{2,1,0:T(8,128)S(1)}, f32[4,264,256]{2,1,0:T(8,128)}, u32[]{:S(2)}) %copy-start) | copy-done | bytes 1081368
  39.2 30.4 %shard_map.140 = f32[2880,128]{1,0:T(8,128)S(1)} custom-call(f32[4,264,256]{2,1,0:T(8,128)S(1)} %copy-done, f32[32]{0:T(128)} %sinks_hbm.3, f32[1,2880]{1,0:T(1,128)S(1)} %reshape.23.bias, bf16[2880,2048]{1,0:T(8,128)(2,1)} %bitcast.19), custom_call_target="tpu_custom_call" | custom-call | flops 400000000 | bytes 16000000 | tf_op jit(solution)/shard_map/pallas_call | solution.py:440
  69.6 0.0 copy-done.1
  69.6 1.0 %fusion = bf16[128,2880]{0,1:T(8,128)(2,1)} fusion(f32[2880,128]{1,0:T(8,128)S(1)} %shard_map.140, bf16[128,2880]{0,1:T(8,128)(2,1)S(1)} %copy-done.1), kind=kLoop, calls=%fused_computation.1 | loop fusion | flops 1105920 | bytes 2949120 | tf_op jit(solution)/shard_map/transpose | solution.py:470
Async XLA Ops:
  2.6 67.0 %copy-start.1 = (bf16[128,2880]{0,1:T(8,128)(2,1)S(1)}, bf16[128,2880]{0,1:T(8,128)(2,1)}, u32[]{:S(2)}) copy-start(bf16[128,2880]{0,1:T(8,128)(2,1)} %param.12) | copy-start | bytes 2211844
  37.9 1.2 %copy-start = (f32[4,264,256]{2,1,0:T(8,128)S(1)}, f32[4,264,256]{2,1,0:T(8,128)}, u32[]{:S(2)}) copy-start(f32[4,264,256]{2,1,0:T(8,128)} %get-tuple-element.6.part) | copy-start | bytes 3244036

commit v2 on v1

--- a/solution.py
+++ b/solution.py
@@ -7,60 +7,84 @@
 from jax.experimental.pallas import tpu as pltpu
 
 NORM_EPS = 1e-5
-CHUNK = 8
+CHUNK = 32
 GROUP = 32
-ROWS = 512
+PIECE = 8
+AHEAD = 2
+PITCH = 136
+NEW = 4
+PARTS = 6
 MESH = pl.DeviceIdType.MESH
 
 
 def attend_kernel(lens_hbm, sinks_hbm, x_hbm, gain_hbm, w_hbm, b_hbm, cos_hbm, sin_hbm, k_hbm, v_hbm,
                   k_out, v_out, part,
-                  lens, sinks, x_t, gain, b_qkv, cos_t, sin_t,
+                  lens, sinks, todo, x_t, gain, b_qkv, cos_t, sin_t,
                   w_buf, w_f32, acc, h_buf, q_buf, kn_t, vn_t, k_buf, v_buf, e_buf,
                   small_sem, w_sem, in_sem, out_sem):
     d_model, seqs = x_t.shape
     n_chunks = seqs // CHUNK
-    n_full, tail = divmod(d_model, ROWS)
+    n_pieces = seqs // PIECE
+    rows_in = d_model // PARTS
 
     smalls = [pltpu.make_async_copy(src, dst, small_sem.at[i]) for i, (src, dst) in enumerate(
         [(x_hbm, x_t), (gain_hbm, gain), (b_hbm, b_qkv), (cos_hbm, cos_t), (sin_hbm, sin_t), (lens_hbm, lens), (sinks_hbm, sinks)])]
     for c in smalls:
         c.start()
 
-    def w_copies(i, n):
-        rows = pl.ds(i * ROWS, n)
-        return [pltpu.make_async_copy(w_hbm.at[rows, :, pl.ds(c * 128, 128)], w_buf.at[c, rows], w_sem.at[i, c]) for c in range(5)]
-
-    for i in range(n_full):
-        for c in w_copies(i, ROWS):
-            c.start()
-    for c in w_copies(n_full, tail):
-        c.start()
+    def w_copy(i, c):
+        rows = pl.ds(i * rows_in, rows_in)
+        return pltpu.make_async_copy(w_hbm.at[rows, :, pl.ds(pl.multiple_of(c * 128, 128), 128)], w_buf.at[c, rows], w_sem.at[i, c])
+
+    def each(n, fn):
+        def step(i, carry):
+            fn(i)
+            return carry
+        lax.fori_loop(0, n, step, 0)
+
+    def start_w(i):
+        each(5, lambda c: w_copy(i, c).start())
+
+    each(AHEAD, start_w)
 
     def cache_in(a, i):
-        rows = pl.ds(i * CHUNK, CHUNK)
+        rows = pl.ds(i * PIECE, PIECE)
         src, dst = ((k_hbm, k_buf), (v_hbm, v_buf))[a]
         return pltpu.make_async_copy(src.at[rows], dst.at[rows], in_sem.at[a, i])
 
     def cache_out(a, i):
-        rows = pl.ds(i * CHUNK, CHUNK)
+        rows = pl.ds(i * PIECE, PIECE)
         src, dst = ((k_buf, k_out), (v_buf, v_out))[a]
         return pltpu.make_async_copy(src.at[rows], dst.at[rows], out_sem.at[a, i])
 
     for c in smalls:
         c.wait()
 
-    sq = jnp.zeros((seqs, 1), jnp.float32)
-    xs = []
-    for j in range(0, d_model, 128):
-        n = min(128, d_model - j)
-        xb = x_t[j:j + n, :].astype(jnp.float32).T
-        xs.append(xb)
-        sq = sq + jnp.sum(xb * xb, axis=1, keepdims=True)
-    inv = lax.rsqrt(sq * (1.0 / d_model) + NORM_EPS)
-    for i, j in enumerate(range(0, d_model, 128)):
-        n = min(128, d_model - j)
-        h_buf[:, j:j + n] = (xs[i] * inv * gain[0:1, j:j + n]).astype(jnp.bfloat16)
+    base = lax.axis_index("sp") * 128
+
+    def note(b, count):
+        loc = lens[b] - base
+        inside = (loc >= 0) & (loc < 128)
+        todo[count] = b
+        return count + jnp.where(inside, 1, 0)
+
+    n_new = lax.fori_loop(0, seqs, note, 0)
+    last = todo[jnp.maximum(n_new - 1, 0)]
+    for u in range(NEW):
+        todo[n_new + u] = last
+
+    def sq_step(i, total):
+        xb = x_t[pl.ds(pl.multiple_of(i * rows_in, rows_in), rows_in), :].astype(jnp.float32)
+        return total + jnp.sum((xb * xb).reshape(rows_in // 8, 8, seqs), axis=0)
+
+    sq = jnp.sum(lax.fori_loop(0, PARTS, sq_step, jnp.zeros((8, seqs), jnp.float32)), axis=0, keepdims=True)
+    inv = jnp.broadcast_to(lax.rsqrt(sq * (1.0 / d_model) + NORM_EPS), (seqs, seqs)).T[:, 0:1]
+
+    def norm_step(i):
+        xb = x_t[pl.ds(pl.multiple_of(i * rows_in, rows_in), rows_in), :].astype(jnp.float32).T
+        h_buf[i] = (xb * inv * gain[i]).astype(jnp.bfloat16)
+
+    each(PARTS, norm_step)
 
     bias = b_qkv[...].astype(jnp.float32)
     for p in range(2):
@@ -68,33 +92,32 @@
             for u in range(2):
                 acc[p, c, :, u * 128:u * 128 + 128] = jnp.broadcast_to(bias[2 * p + u:2 * p + u + 1, c * 128:c * 128 + 128], (seqs, 128))
 
-    def project(i, n):
-        rows = pl.multiple_of(i * ROWS, ROWS)
-        h = h_buf[:, pl.ds(rows, n)]
-        for c, copy in enumerate(w_copies(i, n)):
-            copy.wait()
+    def project(i):
+        @pl.when(i + AHEAD < PARTS)
+        def _():
+            start_w(i + AHEAD)
+
+        @pl.when(i < 2)
+        def _():
+            each(n_pieces // 2, lambda u: cache_in(0, i * (n_pieces // 2) + u).start())
+
+        @pl.when((i >= 2) & (i < 4))
+        def _():
+            each(n_pieces // 2, lambda u: cache_in(1, (i - 2) * (n_pieces // 2) + u).start())
+
+        each(5, lambda c: w_copy(i, c).wait())
+        rows = i * rows_in
+
+        def column(c):
+            w_f32[c % 2] = w_buf[c, pl.ds(rows, rows_in)].reshape(4 * rows_in, 128).astype(jnp.float32)
+            for p in range(2):
+                w = jnp.concatenate([w_f32[c % 2, pl.ds(2 * p + u, rows_in, stride=4), :].astype(jnp.bfloat16) for u in range(2)], axis=1)
+                acc[p, c] += jnp.dot(h_buf[i], w, preferred_element_type=jnp.float32)
+
         for c in range(5):
-            w_f32[c, 0:4 * n, :] = w_buf[c, pl.ds(rows, n)].reshape(4 * n, 128).astype(jnp.float32)
-            for p in range(2):
-                w = jnp.concatenate([w_f32[c, pl.ds(2 * p + u, n, stride=4), :].astype(jnp.bfloat16) for u in range(2)], axis=1)
-                acc[p, c] += jnp.dot(h, w, preferred_element_type=jnp.float32)
-
-    def project_step(i, carry):
-        project(i, ROWS)
-
-        @pl.when(i == 2)
-        def _():
-            for ch in range(n_chunks):
-                cache_in(0, ch).start()
-
-        @pl.when(i == 4)
-        def _():
-            for ch in range(n_chunks):
-                cache_in(1, ch).start()
-        return carry
-
-    lax.fori_loop(0, n_full, project_step, 0)
-    project(n_full, tail)
+            column(c)
+
+    each(PARTS, project)
 
     lane = lax.broadcasted_iota(jnp.int32, (seqs, 128), 1)
     low = lane < 64
@@ -107,21 +130,23 @@
         other = jnp.where(first_half, pltpu.roll(t, 96, 1), pltpu.roll(t, 32, 1))
         return t * cos4 + other * sin4
 
+    def halves(p, tile):
+        t0 = acc[p, tile, :, 0:128]
+        t1 = acc[p, tile, :, 128:256]
+        return jnp.where(low, t0, pltpu.roll(t1, 64, 1)), jnp.where(low, pltpu.roll(t0, 64, 1), t1)
+
     for p in range(2):
+        def q_step(tile):
+            even, odd = halves(p, tile)
+            q_buf[p, pl.ds(pl.multiple_of(2 * tile * PITCH, 8), seqs), :] = rotate(even)
+            q_buf[p, pl.ds(pl.multiple_of((2 * tile + 1) * PITCH, 8), seqs), :] = rotate(odd)
+
+        each(4, q_step)
+        even, odd = halves(p, 4)
         lanes = slice(p * 128, p * 128 + 128)
-        for tile in range(5):
-            t0 = acc[p, tile, :, 0:128]
-            t1 = acc[p, tile, :, 128:256]
-            even = jnp.where(low, t0, pltpu.roll(t1, 64, 1))
-            odd = jnp.where(low, pltpu.roll(t0, 64, 1), t1)
-            if tile < 4:
-                q_buf[p, pl.ds(2 * tile, seqs, stride=8), :] = rotate(even)
-                q_buf[p, pl.ds(2 * tile + 1, seqs, stride=8), :] = rotate(odd)
-            else:
-                kn_t[lanes, :] = rotate(even).T
-                vn_t[lanes, :] = odd.T
-
-    base = lax.axis_index("sp") * 128
+        kn_t[lanes, :] = rotate(even).T.astype(jnp.bfloat16)
+        vn_t[lanes, :] = odd.T.astype(jnp.bfloat16)
+
     lane8 = lax.broadcasted_iota(jnp.int32, (8, 128), 1)
     row8 = lax.broadcasted_iota(jnp.int32, (8, 128), 0)
     sink_rows = []
@@ -130,37 +155,43 @@
         for g in range(8):
             t = jnp.where(row8 == g, sinks[k * 8 + g], t)
         sink_rows.append(t)
-    sink_col = jnp.concatenate(sink_rows, axis=0)[:, 0:1]
+    sink_all = jnp.concatenate(sink_rows, axis=0)
     lane32 = lax.broadcasted_iota(jnp.int32, (32, 128), 1)
     lane256 = lax.broadcasted_iota(jnp.int32, (256, 128), 1)
     q_lane = lax.broadcasted_iota(jnp.int32, (8, 256), 1) // 64
     half8 = lane8 < 64
 
-    def put_new(buf, new_t, i):
-        for u in range(CHUNK):
-            b = i * CHUNK + u
-            loc = lens[b] - base
-
-            @pl.when((loc >= 0) & (loc < 128))
-            def _():
-                shift = lax.rem(loc - b + 256, 128)
-                buf[b] = jnp.where(lane256 == loc, pltpu.roll(new_t[...], shift, 1), buf[b].astype(jnp.float32)).astype(jnp.bfloat16)
+    def put_new(buf, new_t):
+        def step(t, carry):
+            new = []
+            for u in range(NEW):
+                b = todo[t * NEW + u]
+                loc = lens[b] - base
+                col = pltpu.roll(new_t[...], lax.rem(loc - b + 256, 128), 1)
+                new.append((b, jnp.where(lane256 == loc, col, buf[b])))
+            for b, tile in new:
+                buf[b] = tile
+            return carry
+
+        lax.fori_loop(0, (n_new + NEW - 1) // NEW, step, 0)
+
+    def finish(a, buf, new_t):
+        each(n_pieces, lambda i: cache_in(a, i).wait())
+        put_new(buf, new_t)
+        each(n_pieces, lambda i: cache_out(a, i).start())
 
     def score_step(i, carry):
-        cache_in(0, i).wait()
-        put_new(k_buf, kn_t, i)
-        cache_out(0, i).start()
         group = i // (GROUP // CHUNK)
         m_acc = part[group, 256:264, 0:128]
         s_acc = part[group, 256:264, 128:256]
         for u in range(CHUNK):
             b = i * CHUNK + u
             j = lax.rem(i, GROUP // CHUNK) * CHUNK + u
-            rows = jnp.concatenate([q_buf[p, pl.ds(pl.multiple_of(b * 8, 8), 8), :] for p in range(2)], axis=1)
+            rows = jnp.concatenate([q_buf[p, pl.ds(b, 8, stride=PITCH), :] for p in range(2)], axis=1)
             q_blk = jnp.concatenate([jnp.where(q_lane == k, rows, 0.0) for k in range(4)], axis=0).astype(jnp.bfloat16)
             logits = jnp.dot(q_blk, k_buf[b], preferred_element_type=jnp.float32) * 0.125
             logits = jnp.where(lane32 <= lens[b] - base, logits, -jnp.inf)
-            m = jnp.maximum(jnp.max(logits, axis=1, keepdims=True), sink_col)
+            m = jnp.maximum(jnp.broadcast_to(jnp.max(logits, axis=1, keepdims=True), logits.shape), sink_all)
             e = jnp.exp(logits - m)
             s = jnp.sum(e, axis=1, keepdims=True)
             e_buf[pl.ds(pl.multiple_of(b * 32, 32), 32), :] = e.astype(jnp.bfloat16)
@@ -172,12 +203,10 @@
         part[group, 256:264, 128:256] = s_acc
         return carry
 
+    finish(0, k_buf, kn_t)
     lax.fori_loop(0, n_chunks, score_step, 0)
 
     def value_step(i, carry):
-        cache_in(1, i).wait()
-        put_new(v_buf, vn_t, i)
-        cache_out(1, i).start()
         group = i // (GROUP // CHUNK)
         for u in range(CHUNK):
             b = i * CHUNK + u
@@ -189,6 +218,7 @@
             part[group, rows, 128:256] = jnp.where(half8, r[16:24, 128:256], r[24:32, 128:256])
         return carry
 
+    finish(1, v_buf, vn_t)
     lax.fori_loop(0, n_chunks, value_step, 0)
 
     def drain(i, carry):
@@ -196,7 +226,7 @@
         cache_out(1, i).wait()
         return carry
 
-    lax.fori_loop(0, n_chunks, drain, 0)
+    lax.fori_loop(0, n_pieces, drain, 0)
 
 
 def local_attention(hidden, seq_lens, rope_cos, rope_sin, k_cache, v_cache, norm_gain, w_qkv, b_qkv, sink_logits):
@@ -207,7 +237,7 @@
     hbm = lambda a: pltpu.with_memory_space_constraint(a, pltpu.HBM)
     vmem = pl.BlockSpec(memory_space=pltpu.VMEM)
     anyw = pl.BlockSpec(memory_space=pltpu.HBM)
-    n_chunks = seqs // CHUNK
+    n_chunks = seqs // PIECE
     k_out, v_out, part = pl.pallas_call(
         attend_kernel,
         out_shape=(jax.ShapeDtypeStruct(k_t.shape, k_t.dtype), jax.ShapeDtypeStruct(v_t.shape, v_t.dtype),
@@ -217,29 +247,30 @@
         scratch_shapes=[
             pltpu.SMEM((seqs,), jnp.int32),
             pltpu.SMEM((kv * 8,), jnp.float32),
+            pltpu.SMEM((seqs + NEW,), jnp.int32),
             pltpu.VMEM((d_model, seqs), jnp.bfloat16),
-            pltpu.VMEM((1, d_model), jnp.float32),
+            pltpu.VMEM((PARTS, 1, d_model // PARTS), jnp.float32),
             pltpu.VMEM(b_qkv.shape, jnp.bfloat16),
             pltpu.VMEM((dim // 2, seqs), jnp.float32),
             pltpu.VMEM((dim // 2, seqs), jnp.float32),
             pltpu.VMEM((5, d_model, kv, 128), jnp.bfloat16),
-            pltpu.VMEM((5, ROWS * kv, 128), jnp.float32),
+            pltpu.VMEM((2, d_model // PARTS * kv, 128), jnp.float32),
             pltpu.VMEM((2, 5, seqs, 256), jnp.float32),
-            pltpu.VMEM((seqs, 2944), jnp.bfloat16),
-            pltpu.VMEM((2, seqs * 8, 128), jnp.float32),
-            pltpu.VMEM((kv * dim, seqs), jnp.float32),
-            pltpu.VMEM((kv * dim, seqs), jnp.float32),
+            pltpu.VMEM((PARTS, seqs, d_model // PARTS), jnp.bfloat16),
+            pltpu.VMEM((2, 8 * PITCH, 128), jnp.float32),
+            pltpu.VMEM((kv * dim, seqs), jnp.bfloat16),
+            pltpu.VMEM((kv * dim, seqs), jnp.bfloat16),
             pltpu.VMEM(k_t.shape, jnp.bfloat16),
             pltpu.VMEM(v_t.shape, jnp.bfloat16),
             pltpu.VMEM((seqs * 32, 128), jnp.bfloat16),
             pltpu.SemaphoreType.DMA((7,)),
-            pltpu.SemaphoreType.DMA((6, 5)),
+            pltpu.SemaphoreType.DMA((PARTS, 5)),
             pltpu.SemaphoreType.DMA((2, n_chunks)),
             pltpu.SemaphoreType.DMA((2, n_chunks)),
         ],
-        compiler_params=pltpu.CompilerParams(vmem_limit_bytes=56 * 1024 * 1024),
+        compiler_params=pltpu.CompilerParams(vmem_limit_bytes=44 * 1024 * 1024),
         cost_estimate=pl.CostEstimate(flops=3 * 10**9, bytes_accessed=48 * 10**6, transcendentals=10**6),
-    )(hbm(seq_lens), hbm(sink_logits), hbm(hidden.T), norm_gain.astype(jnp.float32)[None, :], hbm(w_qkv), hbm(b_qkv),
+    )(hbm(seq_lens), hbm(sink_logits), hbm(hidden.T), norm_gain.astype(jnp.float32).reshape(PARTS, 1, d_model // PARTS), hbm(w_qkv), hbm(b_qkv),
       hbm(rope_cos.T), hbm(rope_sin.T), hbm(k_t), hbm(v_t))
     back = lambda a: a.reshape(seqs, kv, dim, ctx).transpose(0, 3, 1, 2)
     return back(k_out), back(v_out), part

time: 71.5 us -> 57.9 us (0.81)
  Pallas kernels: 65.7 us -> 54.3 us
  local copies, waits for them, and re-layouts: 3.23 us -> 1.49 us
    pallas_call x1, Pallas kernels: 35.3 us -> 24.1 us  [local_attention(): pl.pallas_call(attend_kernel, out_shape=(jax.ShapeDtypeStruct(k_t.shape,...]
    broadcast_in_dim x1 -> x0, local copies, waits for them, and re-layouts: 1.3 us -> none  [local_attention(): norm_gain.astype(jnp.float32)[None, :]]
    unnamed x4 -> x2, local copies, waits for them, and re-layouts: 1.23 us -> 0.01 us
    reshape x0 -> x1, local copies, waits for them, and re-layouts: none -> 0.78 us  [local_attention(): norm_gain.astype(jnp.float32).reshape(PARTS, 1, d_model // PARTS)]
where the time goes in v2:
time: 57.9 us; the launch traced here: 57.5 us
  Pallas kernels  54.3 us (94%)
  local copies, waits for them, and re-layouts  1.49 us (3%)
  other arithmetic  1.05 us (2%)
  between operations  0.66 us (1%)
    pallas_call x1, Pallas kernels, exchange(): pl.pallas_call(exchange_kernel, out_shape=jax.ShapeDtypeStruct((d_out, 12...  30.3 us
    pallas_call x1, Pallas kernels, local_attention(): pl.pallas_call(attend_kernel, out_shape=(jax.ShapeDtypeStruct(k_t.shape,...  24.1 us

profile of v2, /device:TPU:0, one launch (start us, length us, event | category | flops | bytes accessed | tf_op | source)
XLA Modules:
  0.0 57.5 jit_solution(17983859075857248665)
XLA Ops:
  0.6 0.7 %reshape.31.bias = f32[1,2880]{1,0:T(1,128)S(1)} reshape(bf16[2880]{0:T(1024)(128)(2,1)} %param.23) | data formatting | bytes 17280 | tf_op jit(solution)/shard_map/broadcast_in_dim | solution.py:492
  1.3 0.8 %reshape.30.gain_hbm = f32[6,1,480]{2,1,0:T(1,128)S(1)} reshape(bf16[2880]{0:T(1024)(128)(2,1)} %param.18) | data formatting | bytes 17280 | tf_op jit(solution)/shard_map/reshape | solution.py:273
  2.1 24.1 %shard_map.139 = (bf16[128,256,128]{2,1,0:T(8,128)(2,1)}, bf16[128,256,128]{2,1,0:T(8,128)(2,1)}, f32[4,264,256]{2,1,0:T(8,128)S(1)}) custom-call(s32[128]{0:T(128)} %lens_hbm.1, f32[32]{0:T(128)} %sinks_hbm.3, bf16[2880,128]{1,0:T(8,128)(2,1)} %bitcast.22, f32[6,1,480]{2,1,0:T(1,128)S(1)} %reshape.30.gain_hbm, bf16[2880,4,640]{2,1,0:T(4,128)(2,1)} %w_hbm.1, ...), custom_call_target="tpu_custom_call" | custom-call | flops 3000000000 | bytes 48000000 | tf_op jit(solution)/shard_map/pallas_call | solution.py:241
  26.2 0.0 copy-start
  26.2 30.3 %shard_map.140 = f32[2880,128]{1,0:T(8,128)S(1)} custom-call(f32[4,264,256]{2,1,0:T(8,128)S(1)} %get-tuple-element.6.part, f32[32]{0:T(128)} %sinks_hbm.3, f32[1,2880]{1,0:T(1,128)S(1)} %reshape.31.bias, bf16[2880,2048]{1,0:T(8,128)(2,1)} %bitcast.19), custom_call_target="tpu_custom_call" | custom-call | flops 400000000 | bytes 16000000 | tf_op jit(solution)/shard_map/pallas_call | solution.py:471
  56.5 0.0 copy-done
  56.5 1.1 %fusion = bf16[128,2880]{0,1:T(8,128)(2,1)} fusion(f32[2880,128]{1,0:T(8,128)S(1)} %shard_map.140, bf16[128,2880]{0,1:T(8,128)(2,1)S(1)} %copy-done), kind=kLoop, calls=%fused_computation.1 | loop fusion | flops 1105920 | bytes 2949120 | tf_op jit(solution)/shard_map/transpose | solution.py:501
Async XLA Ops:
  26.2 30.3 %copy-start = (bf16[128,2880]{0,1:T(8,128)(2,1)S(1)}, bf16[128,2880]{0,1:T(8,128)(2,1)}, u32[]{:S(2)}) copy-start(bf16[128,2880]{0,1:T(8,128)(2,1)} %param.12) | copy-start | bytes 2211844

commit v3 on v2

--- a/solution.py
+++ b/solution.py
@@ -7,23 +7,71 @@
 from jax.experimental.pallas import tpu as pltpu
 
 NORM_EPS = 1e-5
-CHUNK = 32
 GROUP = 32
-PIECE = 8
-AHEAD = 2
+PIECE = 16
+AHEAD = 3
 PITCH = 136
 NEW = 4
 PARTS = 6
 MESH = pl.DeviceIdType.MESH
 
 
+def each(n, fn):
+    def step(i, carry):
+        fn(i)
+        return carry
+    lax.fori_loop(0, n, step, 0)
+
+
+def sink_table(sinks):
+    row = lax.broadcasted_iota(jnp.int32, (8, 128), 0)
+    rows = []
+    for k in range(4):
+        t = jnp.zeros((8, 128), jnp.float32)
+        for g in range(8):
+            t = jnp.where(row == g, sinks[k * 8 + g], t)
+        rows.append(t)
+    return rows
+
+
+def score_group(first, base, lens, sink_all, q_buf, keys, e_buf, out):
+    lane8 = lax.broadcasted_iota(jnp.int32, (8, 128), 1)
+    lane32 = lax.broadcasted_iota(jnp.int32, (32, 128), 1)
+    q_lane = lax.broadcasted_iota(jnp.int32, (8, 256), 1) // 64
+    m_acc = jnp.zeros((8, 128), jnp.float32)
+    s_acc = jnp.zeros((8, 128), jnp.float32)
+    for u in range(GROUP):
+        b = first + u
+        rows = jnp.concatenate([q_buf[p, pl.ds(b, 8, stride=PITCH), :] for p in range(2)], axis=1)
+        q_blk = jnp.concatenate([jnp.where(q_lane == k, rows, 0.0) for k in range(4)], axis=0).astype(jnp.bfloat16)
+        logits = jnp.dot(q_blk, keys(u), preferred_element_type=jnp.float32) * 0.125
+        logits = jnp.where(lane32 <= lens[b] - base, logits, -jnp.inf)
+        m = jnp.maximum(jnp.broadcast_to(jnp.max(logits, axis=1, keepdims=True), logits.shape), sink_all)
+        e = jnp.exp(logits - m)
+        s = jnp.sum(e, axis=1, keepdims=True)
+        e_buf[32 * u:32 * u + 32, :] = e.astype(jnp.bfloat16)
+        for k in range(4):
+            here = lane8 == u * 4 + k
+            m_acc = jnp.where(here, m[8 * k:8 * k + 8], m_acc)
+            s_acc = jnp.where(here, s[8 * k:8 * k + 8], s_acc)
+    out[256:264, 0:128] = m_acc
+    out[256:264, 128:256] = s_acc
+
+
+def value_group(values, e_buf, out):
+    half8 = lax.broadcasted_iota(jnp.int32, (8, 128), 1) < 64
+    for u in range(GROUP):
+        r = lax.dot_general(e_buf[32 * u:32 * u + 32, :], values(u), (((1,), (1,)), ((), ())), preferred_element_type=jnp.float32)
+        out[8 * u:8 * u + 8, 0:128] = jnp.where(half8, r[0:8, 0:128], r[8:16, 0:128])
+        out[8 * u:8 * u + 8, 128:256] = jnp.where(half8, r[16:24, 128:256], r[24:32, 128:256])
+
+
 def attend_kernel(lens_hbm, sinks_hbm, x_hbm, gain_hbm, w_hbm, b_hbm, cos_hbm, sin_hbm, k_hbm, v_hbm,
-                  k_out, v_out, part,
+                  k_out, v_out, part, q_buf,
                   lens, sinks, todo, x_t, gain, b_qkv, cos_t, sin_t,
-                  w_buf, w_f32, acc, h_buf, q_buf, kn_t, vn_t, k_buf, v_buf, e_buf,
+                  w_buf, w_f32, acc, h_buf, kn_t, vn_t, k_buf, v_buf, e_buf,
                   small_sem, w_sem, in_sem, out_sem):
     d_model, seqs = x_t.shape
-    n_chunks = seqs // CHUNK
     n_pieces = seqs // PIECE
     rows_in = d_model // PARTS
 
@@ -35,12 +83,6 @@
     def w_copy(i, c):
         rows = pl.ds(i * rows_in, rows_in)
         return pltpu.make_async_copy(w_hbm.at[rows, :, pl.ds(pl.multiple_of(c * 128, 128), 128)], w_buf.at[c, rows], w_sem.at[i, c])
-
-    def each(n, fn):
-        def step(i, carry):
-            fn(i)
-            return carry
-        lax.fori_loop(0, n, step, 0)
 
     def start_w(i):
         each(5, lambda c: w_copy(i, c).start())
@@ -147,20 +189,8 @@
         kn_t[lanes, :] = rotate(even).T.astype(jnp.bfloat16)
         vn_t[lanes, :] = odd.T.astype(jnp.bfloat16)
 
-    lane8 = lax.broadcasted_iota(jnp.int32, (8, 128), 1)
-    row8 = lax.broadcasted_iota(jnp.int32, (8, 128), 0)
-    sink_rows = []
-    for k in range(4):
-        t = jnp.zeros((8, 128), jnp.float32)
-        for g in range(8):
-            t = jnp.where(row8 == g, sinks[k * 8 + g], t)
-        sink_rows.append(t)
-    sink_all = jnp.concatenate(sink_rows, axis=0)
-    lane32 = lax.broadcasted_iota(jnp.int32, (32, 128), 1)
+    sink_all = jnp.concatenate(sink_table(sinks), axis=0)
     lane256 = lax.broadcasted_iota(jnp.int32, (256, 128), 1)
-    q_lane = lax.broadcasted_iota(jnp.int32, (8, 256), 1) // 64
-    half8 = lane8 < 64
-
     def put_new(buf, new_t):
         def step(t, carry):
             new = []
@@ -180,46 +210,21 @@
         put_new(buf, new_t)
         each(n_pieces, lambda i: cache_out(a, i).start())
 
-    def score_step(i, carry):
-        group = i // (GROUP // CHUNK)
-        m_acc = part[group, 256:264, 0:128]
-        s_acc = part[group, 256:264, 128:256]
-        for u in range(CHUNK):
-            b = i * CHUNK + u
-            j = lax.rem(i, GROUP // CHUNK) * CHUNK + u
-            rows = jnp.concatenate([q_buf[p, pl.ds(b, 8, stride=PITCH), :] for p in range(2)], axis=1)
-            q_blk = jnp.concatenate([jnp.where(q_lane == k, rows, 0.0) for k in range(4)], axis=0).astype(jnp.bfloat16)
-            logits = jnp.dot(q_blk, k_buf[b], preferred_element_type=jnp.float32) * 0.125
-            logits = jnp.where(lane32 <= lens[b] - base, logits, -jnp.inf)
-            m = jnp.maximum(jnp.broadcast_to(jnp.max(logits, axis=1, keepdims=True), logits.shape), sink_all)
-            e = jnp.exp(logits - m)
-            s = jnp.sum(e, axis=1, keepdims=True)
-            e_buf[pl.ds(pl.multiple_of(b * 32, 32), 32), :] = e.astype(jnp.bfloat16)
-            for k in range(4):
-                here = lane8 == j * 4 + k
-                m_acc = jnp.where(here, m[8 * k:8 * k + 8], m_acc)
-                s_acc = jnp.where(here, s[8 * k:8 * k + 8], s_acc)
-        part[group, 256:264, 0:128] = m_acc
-        part[group, 256:264, 128:256] = s_acc
-        return carry
-
+    away = (1 - lax.axis_index("sp") // 2) * 2 * GROUP
     finish(0, k_buf, kn_t)
-    lax.fori_loop(0, n_chunks, score_step, 0)
-
-    def value_step(i, carry):
-        group = i // (GROUP // CHUNK)
-        for u in range(CHUNK):
-            b = i * CHUNK + u
-            j = lax.rem(i, GROUP // CHUNK) * CHUNK + u
-            e = e_buf[pl.ds(pl.multiple_of(b * 32, 32), 32), :]
-            r = lax.dot_general(e, v_buf[b], (((1,), (1,)), ((), ())), preferred_element_type=jnp.float32)
-            rows = pl.ds(pl.multiple_of(j * 8, 8), 8)
-            part[group, rows, 0:128] = jnp.where(half8, r[0:8, 0:128], r[8:16, 0:128])
-            part[group, rows, 128:256] = jnp.where(half8, r[16:24, 128:256], r[24:32, 128:256])
-        return carry
-
+
+    def score_away(t):
+        first = away + t * GROUP
+        score_group(first, base, lens, sink_all, q_buf, lambda u: k_buf[first + u], e_buf.at[t], part.at[t])
+
+    each(2, score_away)
     finish(1, v_buf, vn_t)
-    lax.fori_loop(0, n_chunks, value_step, 0)
+
+    def value_away(t):
+        first = away + t * GROUP
+        value_group(lambda u: v_buf[first + u], e_buf.at[t], part.at[t])
+
+    each(2, value_away)
 
     def drain(i, carry):
         cache_out(0, i).wait()
@@ -238,12 +243,13 @@
     vmem = pl.BlockSpec(memory_space=pltpu.VMEM)
     anyw = pl.BlockSpec(memory_space=pltpu.HBM)
     n_chunks = seqs // PIECE
-    k_out, v_out, part = pl.pallas_call(
+    k_out, v_out, part, q_buf = pl.pallas_call(
         attend_kernel,
         out_shape=(jax.ShapeDtypeStruct(k_t.shape, k_t.dtype), jax.ShapeDtypeStruct(v_t.shape, v_t.dtype),
-                   jax.ShapeDtypeStruct((seqs // GROUP, GROUP * 8 + 8, kv * dim), jnp.float32)),
+                   jax.ShapeDtypeStruct((2, GROUP * 8 + 8, kv * dim), jnp.float32),
+                   jax.ShapeDtypeStruct((2, 8 * PITCH, 128), jnp.float32)),
         in_specs=[anyw] * 10,
-        out_specs=(anyw, anyw, vmem),
+        out_specs=(anyw, anyw, vmem, vmem),
         scratch_shapes=[
             pltpu.SMEM((seqs,), jnp.int32),
             pltpu.SMEM((kv * 8,), jnp.float32),
@@ -257,12 +263,11 @@
             pltpu.VMEM((2, d_model // PARTS * kv, 128), jnp.float32),
             pltpu.VMEM((2, 5, seqs, 256), jnp.float32),
             pltpu.VMEM((PARTS, seqs, d_model // PARTS), jnp.bfloat16),
-            pltpu.VMEM((2, 8 * PITCH, 128), jnp.float32),
             pltpu.VMEM((kv * dim, seqs), jnp.bfloat16),
             pltpu.VMEM((kv * dim, seqs), jnp.bfloat16),
             pltpu.VMEM(k_t.shape, jnp.bfloat16),
             pltpu.VMEM(v_t.shape, jnp.bfloat16),
-            pltpu.VMEM((seqs * 32, 128), jnp.bfloat16),
+            pltpu.VMEM((2, GROUP * 32, 128), jnp.bfloat16),
             pltpu.SemaphoreType.DMA((7,)),
             pltpu.SemaphoreType.DMA((PARTS, 5)),
             pltpu.SemaphoreType.DMA((2, n_chunks)),
@@ -272,17 +277,16 @@
         cost_estimate=pl.CostEstimate(flops=3 * 10**9, bytes_accessed=48 * 10**6, transcendentals=10**6),
     )(hbm(seq_lens), hbm(sink_logits), hbm(hidden.T), norm_gain.astype(jnp.float32).reshape(PARTS, 1, d_model // PARTS), hbm(w_qkv), hbm(b_qkv),
       hbm(rope_cos.T), hbm(rope_sin.T), hbm(k_t), hbm(v_t))
-    back = lambda a: a.reshape(seqs, kv, dim, ctx).transpose(0, 3, 1, 2)
-    return back(k_out), back(v_out), part
+    return k_out, v_out, part, q_buf
 
 
 COLS = 512
 HALF = 3 * COLS
 
 
-def exchange_kernel(part, sinks_hbm, bias, w_hbm, y_out,
-                    sinks, w_buf, from_core, to_chip, own, from_chip, o_buf, lhs, y_buf, from_tp, gather,
-                    small_sem, w_sem, core_send, core_recv, chip_send, chip_recv, tp_send, tp_recv, ag_send, ag_recv):
+def exchange_kernel(part, q_buf, k_hbm, v_hbm, lens_hbm, sinks_hbm, bias, w_hbm, y_out,
+                    lens, sinks, k_buf, v_buf, e_buf, mine_part, w_buf, from_core, to_chip, own, from_chip, o_buf, lhs, y_buf, from_tp, gather,
+                    small_sem, kv_sem, w_sem, core_send, core_recv, chip_send, chip_recv, tp_send, tp_recv, ag_send, ag_recv):
     tp = lax.axis_index("tp")
     sp = lax.axis_index("sp")
     core = lax.rem(sp, 2)
@@ -293,8 +297,12 @@
     across_x = {"sp": lax.rem(sp + 2, 4)}
     across_y = {"tp": 1 - tp}
 
-    small = pltpu.make_async_copy(sinks_hbm, sinks, small_sem)
-    small.start()
+    smalls = [pltpu.make_async_copy(sinks_hbm, sinks, small_sem.at[0]), pltpu.make_async_copy(lens_hbm, lens, small_sem.at[1])]
+    first_own = pl.multiple_of(chip * 2 * GROUP, GROUP)
+    kv_copies = [[pltpu.make_async_copy(src.at[pl.ds(first_own + t * GROUP, GROUP)], dst.at[pl.ds(t * GROUP, GROUP)], kv_sem.at[a, t]) for t in range(2)]
+                 for a, (src, dst) in enumerate(((k_hbm, k_buf), (v_hbm, v_buf)))]
+    for c in smalls + kv_copies[0] + kv_copies[1]:
+        c.start()
     w_copies = [pltpu.make_async_copy(w_hbm.at[pl.ds(n, w)], w_buf.at[pl.ds(n, w)], w_sem.at[i]) for i, (n, w) in enumerate(n_cols)]
     for c in w_copies:
         c.start()
@@ -307,16 +315,19 @@
     def remote(src, dst, ss, rs, peer):
         return pltpu.make_async_remote_copy(src_ref=src, dst_ref=dst, send_sem=ss, recv_sem=rs, device_id=peer, device_id_type=MESH)
 
-    core_copies = []
-    for r in range(2):
-        x_side = (1 - chip) if r == 0 else chip
-        group = 2 * x_side + (1 - core)
-        core_copies.append(remote(part.at[group], from_core.at[r], core_send.at[r], core_recv.at[r], sibling))
-    for c in core_copies:
-        c.start()
+    pieces = [(0, 8), (8, 16), (16, 24), (24, 32)]
+    order = [3, 0, 1, 2]
+
+    def piece_rows(i):
+        j0, j1 = pieces[i]
+        return pl.ds(8 * j0, 8 * (j1 - j0) + (8 if i == len(pieces) - 1 else 0))
+
+    away_theirs = part.at[1 - core]
+    core_copies = [remote(away_theirs.at[piece_rows(i)], from_core.at[0, piece_rows(i)], core_send.at[i], core_recv.at[i], sibling) for i in range(4)]
+    for i in order:
+        core_copies[i].start()
 
     lane = lax.broadcasted_iota(jnp.int32, (8, 128), 1)
-    row = lax.broadcasted_iota(jnp.int32, (8, 128), 0)
     high = lane // 64
 
     def spread(f, j, p):
@@ -340,34 +351,40 @@
                 cols = slice(128 * p, 128 * p + 128)
                 out_ref[rows, cols] = a_ref[rows, cols] * spread(f_a, j, p) + b_ref[rows, cols] * spread(f_b, j, p)
 
-    pieces = [(0, 8), (8, 16), (16, 24), (24, 32)]
-
-    def piece_rows(i):
-        j0, j1 = pieces[i]
-        return pl.ds(8 * j0, 8 * (j1 - j0) + (8 if i == len(pieces) - 1 else 0))
-
-    core_copies[0].wait_recv()
-    away = part.at[2 * (1 - chip) + core]
+    core_copies[3].wait_recv()
+    away = part.at[core]
     m, s, f_a, f_b = stats(stat_rows(away), stat_rows(from_core.at[0]))
     to_chip[256:264, 0:128] = m
     to_chip[256:264, 128:256] = s
     chip_copies = [remote(to_chip.at[piece_rows(i)], from_chip.at[piece_rows(i)], chip_send.at[i], chip_recv.at[i], across_x) for i in range(len(pieces))]
-    order = [3, 0, 1, 2]
     for i in order:
+        if i != 3:
+            core_copies[i].wait_recv()
         merge(away, from_core.at[0], to_chip, f_a, f_b, *pieces[i])
         chip_copies[i].start()
 
-    core_copies[1].wait_recv()
-    here = part.at[2 * chip + core]
+    for c in smalls:
+        c.wait()
+    base = sp * 128
+    sink_rows = sink_table(sinks)
+    sink_all = jnp.concatenate(sink_rows, axis=0)
+    for c in kv_copies[0]:
+        c.wait()
+    each(2, lambda t: score_group(first_own + t * GROUP, base, lens, sink_all, q_buf, lambda u: k_buf[t * GROUP + u], e_buf.at[t], mine_part.at[t]))
+    for c in kv_copies[1]:
+        c.wait()
+    each(2, lambda t: value_group(lambda u: v_buf[t * GROUP + u], e_buf.at[t], mine_part.at[t]))
+    core_copies.append(remote(mine_part.at[1 - core], from_core.at[1], core_send.at[4], core_recv.at[4], sibling))
+    core_copies[4].start()
+
+    sink = sink_rows[3]
+    for k in range(3):
+        sink = jnp.where((lane & 3) == k, sink_rows[k], sink)
+
+    core_copies[4].wait_recv()
+    here = mine_part.at[core]
     m_own, s_own, f_a, f_b = stats(stat_rows(here), stat_rows(from_core.at[1]))
     merge(here, from_core.at[1], own, f_a, f_b, 0, 32)
-
-    small.wait()
-    sink = jnp.zeros((8, 128), jnp.float32)
-    k_of_lane = lane & 3
-    for k in range(4):
-        for g in range(8):
-            sink = jnp.where((row == g) & (k_of_lane == k), sinks[k * 8 + g], sink)
 
     chip_copies[3].wait_recv()
     m, s, f_a, f_b = stats((m_own, s_own), stat_rows(from_chip))
@@ -458,7 +475,7 @@
         c.wait_send()
 
 
-def exchange(part, sink_logits, w_o, b_o):
+def exchange(part, q_buf, k_out, v_out, seq_lens, sink_logits, w_o, b_o):
     d_out = w_o.shape[1]
     heads = w_o.shape[0]
     n_col = -(-d_out // COLS)
@@ -471,10 +488,15 @@
     return pl.pallas_call(
         exchange_kernel,
         out_shape=jax.ShapeDtypeStruct((d_out, 128), jnp.float32),
-        in_specs=[vmem, anyw, vmem, anyw],
+        in_specs=[vmem, vmem, anyw, anyw, anyw, anyw, vmem, anyw],
         out_specs=vmem,
         scratch_shapes=[
+            pltpu.SMEM(seq_lens.shape, jnp.int32),
             pltpu.SMEM(sink_logits.shape, jnp.float32),
+            pltpu.VMEM((2 * GROUP,) + k_out.shape[1:], jnp.bfloat16),
+            pltpu.VMEM((2 * GROUP,) + k_out.shape[1:], jnp.bfloat16),
+            pltpu.VMEM((2, GROUP * 32, 128), jnp.bfloat16),
+            pltpu.VMEM((2,) + block, jnp.float32),
             pltpu.VMEM((d_out, heads), jnp.bfloat16),
             pltpu.VMEM((2,) + block, jnp.float32),
             pltpu.VMEM(block, jnp.float32),
@@ -485,20 +507,22 @@
             pltpu.VMEM((n_col, 32, COLS), jnp.float32),
             pltpu.VMEM((n_col, 16, COLS), jnp.float32),
             pltpu.VMEM((128, padded), jnp.float32),
-            dma, dma((n_col,)), dma((2,)), dma((2,)), dma((4,)), dma((4,)), dma((n_col,)), dma((n_col,)), dma((7, 2)), dma((7, 2)),
+            dma((2,)), dma((2, 2)), dma((n_col,)), dma((5,)), dma((5,)), dma((4,)), dma((4,)), dma((n_col,)), dma((n_col,)), dma((7, 2)), dma((7, 2)),
         ],
-        compiler_params=pltpu.CompilerParams(collective_id=0, has_side_effects=True, vmem_limit_bytes=32 * 1024 * 1024),
+        compiler_params=pltpu.CompilerParams(collective_id=0, has_side_effects=True, vmem_limit_bytes=40 * 1024 * 1024),
         cost_estimate=pl.CostEstimate(flops=4 * 10**8, bytes_accessed=16 * 10**6, transcendentals=10**5),
-    )(part, hbm(sink_logits), b_o.astype(jnp.float32)[None, :], hbm(w_o.T))
+      )(part, q_buf, hbm(k_out), hbm(v_out), hbm(seq_lens), hbm(sink_logits), b_o.astype(jnp.float32)[None, :], hbm(w_o.T))
 
 
 def solution(mesh):
     cache_spec = P("dp", "sp", "tp", None)
 
     def block_step(hidden, seq_lens, rope_cos, rope_sin, k_cache, v_cache, norm_gain, w_qkv, b_qkv, sink_logits, w_o, b_o):
-        k_out, v_out, part = local_attention(hidden, seq_lens, rope_cos, rope_sin, k_cache, v_cache, norm_gain, w_qkv, b_qkv, sink_logits)
-        y_t = exchange(part, sink_logits, w_o, b_o)
+        k_out, v_out, part, q_buf = local_attention(hidden, seq_lens, rope_cos, rope_sin, k_cache, v_cache, norm_gain, w_qkv, b_qkv, sink_logits)
+        y_t = exchange(part, q_buf, k_out, v_out, seq_lens, sink_logits, w_o, b_o)
         out_hidden = (hidden.T.astype(jnp.float32) + y_t).astype(jnp.bfloat16).T
-        return out_hidden, k_out, v_out
+        seqs, ctx, kv, dim = k_cache.shape
+        back = lambda a: a.reshape(seqs, kv, dim, ctx).transpose(0, 3, 1, 2)
+        return out_hidden, back(k_out), back(v_out)
 
     return jax.shard_map(block_step, mesh=mesh, in_specs=(P("dp", None), P("dp"), P("dp", None), P("dp", None), cache_spec, cache_spec, P(None), P(None, "tp", None), P("tp", None), P("tp"), P("tp", None), P(None)), out_specs=(P("dp", None), cache_spec, cache_spec), check_vma=False)

time: 57.9 us -> 55.6 us (0.960)
  Pallas kernels: 54.3 us -> 52 us
    pallas_call x1, Pallas kernels: 24.1 us -> 21.7 us  [local_attention(): pl.pallas_call(attend_kernel, out_shape=(jax.ShapeDtypeStruct(k_t.shape,...]
where the time goes in v3:
time: 55.6 us; the launch traced here: 55.1 us
  Pallas kernels  52 us (94%)
  local copies, waits for them, and re-layouts  1.49 us (3%)
  other arithmetic  1.01 us (2%)
  between operations  0.66 us (1%)
    pallas_call x1, Pallas kernels, exchange(): pl.pallas_call(exchange_kernel, out_shape=jax.ShapeDtypeStruct((d_out, 12...  30.2 us
    pallas_call x1, Pallas kernels, local_attention(): pl.pallas_call(attend_kernel, out_shape=(jax.ShapeDtypeStruct(k_t.shape,...  21.7 us

profile of v3, /device:TPU:0, one launch (start us, length us, event | category | flops | bytes accessed | tf_op | source)
XLA Modules:
  0.0 55.1 jit_solution(2906278477328800363)
XLA Ops:
  0.6 0.7 %reshape.31.bias = f32[1,2880]{1,0:T(1,128)S(1)} reshape(bf16[2880]{0:T(1024)(128)(2,1)} %param.23) | data formatting | bytes 17280 | tf_op jit(solution)/shard_map/broadcast_in_dim | solution.py:514
  1.3 0.8 %reshape.30.gain_hbm = f32[6,1,480]{2,1,0:T(1,128)S(1)} reshape(bf16[2880]{0:T(1024)(128)(2,1)} %param.18) | data formatting | bytes 17280 | tf_op jit(solution)/shard_map/reshape | solution.py:278
  2.1 21.7 %shard_map.139 = (bf16[128,256,128]{2,1,0:T(8,128)(2,1)}, bf16[128,256,128]{2,1,0:T(8,128)(2,1)}, f32[2,264,256]{2,1,0:T(8,128)S(1)}, f32[2,1088,128]{2,1,0:T(8,128)S(1)}) custom-call(s32[128]{0:T(128)} %lens_hbm.3, f32[32]{0:T(128)} %sinks_hbm.3, bf16[2880,128]{1,0:T(8,128)(2,1)} %bitcast.24, f32[6,1,480]{2,1,0:T(1,128)S(1)} %reshape.30.gain_hbm, ...), custom_call_target="tpu_custom_call" | custom-call | flops 3000000000 | bytes 48000000 | tf_op jit(solution)/shard_map/pallas_call | solution.py:246
  23.9 0.0 copy-start
  23.9 30.2 %shard_map.140 = f32[2880,128]{1,0:T(8,128)S(1)} custom-call(f32[2,264,256]{2,1,0:T(8,128)S(1)} %get-tuple-element.7.part, f32[2,1088,128]{2,1,0:T(8,128)S(1)} %get-tuple-element.8.q_buf, bf16[128,256,128]{2,1,0:T(8,128)(2,1)} %get-tuple-element.9.k_hbm, bf16[128,256,128]{2,1,0:T(8,128)(2,1)} %get-tuple-element.10.v_hbm, s32[128]{0:T(128)} %lens_hbm.3, ...), custom_call_target="tpu_custom_call" | custom-call | flops 400000000 | bytes 16000000 | tf_op jit(solution)/shard_map/pallas_call | solution.py:488
  54.1 0.0 copy-done
  54.1 1.0 %fusion = bf16[128,2880]{0,1:T(8,128)(2,1)} fusion(f32[2880,128]{1,0:T(8,128)S(1)} %shard_map.140, bf16[128,2880]{0,1:T(8,128)(2,1)S(1)} %copy-done), kind=kLoop, calls=%fused_computation.1 | loop fusion | flops 1105920 | bytes 2949120 | tf_op jit(solution)/shard_map/transpose | solution.py:523
Async XLA Ops:
  23.9 30.3 %copy-start = (bf16[128,2880]{0,1:T(8,128)(2,1)S(1)}, bf16[128,2880]{0,1:T(8,128)(2,1)}, u32[]{:S(2)}) copy-start(bf16[128,2880]{0,1:T(8,128)(2,1)} %param.12) | copy-start | bytes 2211844

commit v4 on v3

--- a/solution.py
+++ b/solution.py
@@ -8,11 +8,16 @@
 
 NORM_EPS = 1e-5
 GROUP = 32
-PIECE = 16
+LANES = 128
+LO = slice(0, LANES)
+HI = slice(LANES, 2 * LANES)
+STAT = slice(8 * GROUP, 8 * GROUP + 8)
+PIECE = 32
 AHEAD = 3
 PITCH = 136
-NEW = 4
+NEW = 8
 PARTS = 6
+BLOCKS = 6
 MESH = pl.DeviceIdType.MESH
 
 
@@ -54,21 +59,21 @@
             here = lane8 == u * 4 + k
             m_acc = jnp.where(here, m[8 * k:8 * k + 8], m_acc)
             s_acc = jnp.where(here, s[8 * k:8 * k + 8], s_acc)
-    out[256:264, 0:128] = m_acc
-    out[256:264, 128:256] = s_acc
+    out[STAT, LO] = m_acc
+    out[STAT, HI] = s_acc
 
 
 def value_group(values, e_buf, out):
     half8 = lax.broadcasted_iota(jnp.int32, (8, 128), 1) < 64
     for u in range(GROUP):
         r = lax.dot_general(e_buf[32 * u:32 * u + 32, :], values(u), (((1,), (1,)), ((), ())), preferred_element_type=jnp.float32)
-        out[8 * u:8 * u + 8, 0:128] = jnp.where(half8, r[0:8, 0:128], r[8:16, 0:128])
-        out[8 * u:8 * u + 8, 128:256] = jnp.where(half8, r[16:24, 128:256], r[24:32, 128:256])
+        out[8 * u:8 * u + 8, LO] = jnp.where(half8, r[0:8, LO], r[8:16, LO])
+        out[8 * u:8 * u + 8, HI] = jnp.where(half8, r[16:24, HI], r[24:32, HI])
 
 
 def attend_kernel(lens_hbm, sinks_hbm, x_hbm, gain_hbm, w_hbm, b_hbm, cos_hbm, sin_hbm, k_hbm, v_hbm,
                   k_out, v_out, part, q_buf,
-                  lens, sinks, todo, x_t, gain, b_qkv, cos_t, sin_t,
+                  lens, sinks, todo, ends, x_t, gain, b_qkv, cos_t, sin_t,
                   w_buf, w_f32, acc, h_buf, kn_t, vn_t, k_buf, v_buf, e_buf,
                   small_sem, w_sem, in_sem, out_sem):
     d_model, seqs = x_t.shape
@@ -104,16 +109,16 @@
 
     base = lax.axis_index("sp") * 128
 
+    ends[0] = 0
+
     def note(b, count):
         loc = lens[b] - base
-        inside = (loc >= 0) & (loc < 128)
         todo[count] = b
-        return count + jnp.where(inside, 1, 0)
-
-    n_new = lax.fori_loop(0, seqs, note, 0)
-    last = todo[jnp.maximum(n_new - 1, 0)]
-    for u in range(NEW):
-        todo[n_new + u] = last
+        count = count + jnp.where((loc >= 0) & (loc < LANES), 1, 0)
+        ends[b // PIECE + 1] = count
+        return count
+
+    lax.fori_loop(0, seqs, note, 0)
 
     def sq_step(i, total):
         xb = x_t[pl.ds(pl.multiple_of(i * rows_in, rows_in), rows_in), :].astype(jnp.float32)
@@ -126,7 +131,6 @@
         xb = x_t[pl.ds(pl.multiple_of(i * rows_in, rows_in), rows_in), :].astype(jnp.float32).T
         h_buf[i] = (xb * inv * gain[i]).astype(jnp.bfloat16)
 
-    each(PARTS, norm_step)
 
     bias = b_qkv[...].astype(jnp.float32)
     for p in range(2):
@@ -147,6 +151,7 @@
         def _():
             each(n_pieces // 2, lambda u: cache_in(1, (i - 2) * (n_pieces // 2) + u).start())
 
+        norm_step(i)
         each(5, lambda c: w_copy(i, c).wait())
         rows = i * rows_in
 
@@ -173,8 +178,8 @@
         return t * cos4 + other * sin4
 
     def halves(p, tile):
-        t0 = acc[p, tile, :, 0:128]
-        t1 = acc[p, tile, :, 128:256]
+        t0 = acc[p, tile, :, LO]
+        t1 = acc[p, tile, :, HI]
         return jnp.where(low, t0, pltpu.roll(t1, 64, 1)), jnp.where(low, pltpu.roll(t0, 64, 1), t1)
 
     for p in range(2):
@@ -191,24 +196,31 @@
 
     sink_all = jnp.concatenate(sink_table(sinks), axis=0)
     lane256 = lax.broadcasted_iota(jnp.int32, (256, 128), 1)
-    def put_new(buf, new_t):
-        def step(t, carry):
-            new = []
-            for u in range(NEW):
-                b = todo[t * NEW + u]
-                loc = lens[b] - base
-                col = pltpu.roll(new_t[...], lax.rem(loc - b + 256, 128), 1)
-                new.append((b, jnp.where(lane256 == loc, col, buf[b])))
-            for b, tile in new:
-                buf[b] = tile
-            return carry
-
-        lax.fori_loop(0, (n_new + NEW - 1) // NEW, step, 0)
-
     def finish(a, buf, new_t):
-        each(n_pieces, lambda i: cache_in(a, i).wait())
-        put_new(buf, new_t)
-        each(n_pieces, lambda i: cache_out(a, i).start())
+        def piece(i):
+            cache_in(a, i).wait()
+
+            @pl.when(i > 0)
+            def _():
+                cache_out(a, i - 1).start()
+
+            begin, end = ends[i], ends[i + 1]
+
+            def step(t, carry):
+                new = []
+                for u in range(NEW):
+                    b = todo[jnp.minimum(begin + t * NEW + u, end - 1)]
+                    loc = lens[b] - base
+                    col = pltpu.roll(new_t[...], lax.rem(loc - b + 2 * LANES, LANES), 1)
+                    new.append((b, jnp.where(lane256 == loc, col, buf[b])))
+                for b, tile in new:
+                    buf[b] = tile
+                return carry
+
+            lax.fori_loop(0, (end - begin + NEW - 1) // NEW, step, 0)
+
+        each(n_pieces, piece)
+        cache_out(a, n_pieces - 1).start()
 
     away = (1 - lax.axis_index("sp") // 2) * 2 * GROUP
     finish(0, k_buf, kn_t)
@@ -254,6 +266,7 @@
             pltpu.SMEM((seqs,), jnp.int32),
             pltpu.SMEM((kv * 8,), jnp.float32),
             pltpu.SMEM((seqs + NEW,), jnp.int32),
+            pltpu.SMEM((seqs // PIECE + 1,), jnp.int32),
             pltpu.VMEM((d_model, seqs), jnp.bfloat16),
             pltpu.VMEM((PARTS, 1, d_model // PARTS), jnp.float32),
             pltpu.VMEM(b_qkv.shape, jnp.bfloat16),
@@ -275,24 +288,20 @@
         ],
         compiler_params=pltpu.CompilerParams(vmem_limit_bytes=44 * 1024 * 1024),
         cost_estimate=pl.CostEstimate(flops=3 * 10**9, bytes_accessed=48 * 10**6, transcendentals=10**6),
-    )(hbm(seq_lens), hbm(sink_logits), hbm(hidden.T), norm_gain.astype(jnp.float32).reshape(PARTS, 1, d_model // PARTS), hbm(w_qkv), hbm(b_qkv),
+    )(hbm(seq_lens), hbm(sink_logits), hbm(hidden.T), norm_gain, hbm(w_qkv), hbm(b_qkv),
       hbm(rope_cos.T), hbm(rope_sin.T), hbm(k_t), hbm(v_t))
     return k_out, v_out, part, q_buf
 
 
-COLS = 512
-HALF = 3 * COLS
-
-
 def exchange_kernel(part, q_buf, k_hbm, v_hbm, lens_hbm, sinks_hbm, bias, w_hbm, y_out,
-                    lens, sinks, k_buf, v_buf, e_buf, mine_part, w_buf, from_core, to_chip, own, from_chip, o_buf, lhs, y_buf, from_tp, gather,
-                    small_sem, kv_sem, w_sem, core_send, core_recv, chip_send, chip_recv, tp_send, tp_recv, ag_send, ag_recv):
+                    lens, sinks, k_buf, v_buf, e_buf, mine_part, w_buf, from_core, to_chip, own, from_chip, o_all, lhs, y_buf, from_tp, gather,
+                    small_sem, kv_sem, w_sem, core_send, core_recv, chip_send, chip_recv, o_send, o_recv, tp_send, tp_recv, ag_send, ag_recv):
     tp = lax.axis_index("tp")
     sp = lax.axis_index("sp")
     core = lax.rem(sp, 2)
     chip = sp // 2
-    d_out = w_hbm.shape[0]
-    n_cols = [(n, min(COLS, d_out - n)) for n in range(0, d_out, COLS)]
+    width = gather.shape[-1]
+    share = w_buf.shape[0]
     sibling = {"sp": sp + 1 - 2 * core}
     across_x = {"sp": lax.rem(sp + 2, 4)}
     across_y = {"tp": 1 - tp}
@@ -303,7 +312,7 @@
                  for a, (src, dst) in enumerate(((k_hbm, k_buf), (v_hbm, v_buf)))]
     for c in smalls + kv_copies[0] + kv_copies[1]:
         c.start()
-    w_copies = [pltpu.make_async_copy(w_hbm.at[pl.ds(n, w)], w_buf.at[pl.ds(n, w)], w_sem.at[i]) for i, (n, w) in enumerate(n_cols)]
+    w_copies = [pltpu.make_async_copy(w_hbm.at[pl.ds((share * core + i) * width, width)], w_buf.at[i], w_sem.at[i]) for i in range(share)]
     for c in w_copies:
         c.start()
 
@@ -342,7 +351,7 @@
         return m, s_a * f_a + s_b * f_b, f_a, f_b
 
     def stat_rows(ref):
-        return ref[256:264, 0:128], ref[256:264, 128:256]
+        return ref[STAT, LO], ref[STAT, HI]
 
     def merge(a_ref, b_ref, out_ref, f_a, f_b, j0, j1):
         for j in range(j0, j1):
@@ -354,8 +363,8 @@
     core_copies[3].wait_recv()
     away = part.at[core]
     m, s, f_a, f_b = stats(stat_rows(away), stat_rows(from_core.at[0]))
-    to_chip[256:264, 0:128] = m
-    to_chip[256:264, 128:256] = s
+    to_chip[STAT, LO] = m
+    to_chip[STAT, HI] = s
     chip_copies = [remote(to_chip.at[piece_rows(i)], from_chip.at[piece_rows(i)], chip_send.at[i], chip_recv.at[i], across_x) for i in range(len(pieces))]
     for i in order:
         if i != 3:
@@ -391,6 +400,7 @@
     scale = 1.0 / (s + jnp.exp(sink - m))
     f_a = f_a * scale
     f_b = f_b * scale
+    o_copies = []
     for i in order:
         if i != 3:
             chip_copies[i].wait_recv()
@@ -398,88 +408,91 @@
             rows = slice(8 * j, 8 * j + 8)
             for p in range(2):
                 cols = slice(128 * p, 128 * p + 128)
-                o_buf[p, rows, :] = own[rows, cols] * spread(f_a, j, p) + from_chip[rows, cols] * spread(f_b, j, p)
-
-    low = lax.broadcasted_iota(jnp.int32, (32, 128), 1) < 64
-    for p in range(2):
-        for t in range(4):
-            a = o_buf[p, pl.ds(2 * t, 32, stride=8), :]
-            b = o_buf[p, pl.ds(2 * t + 1, 32, stride=8), :]
-            even_k = (2 * p) * 512 + t * 128
-            odd_k = (2 * p + 1) * 512 + t * 128
-            lhs[:, even_k:even_k + 128] = jnp.where(low, a, pltpu.roll(b, 64, 1)).astype(jnp.bfloat16)
-            lhs[:, odd_k:odd_k + 128] = jnp.where(low, pltpu.roll(a, 64, 1), b).astype(jnp.bfloat16)
-
-    theirs = pl.ds(pl.multiple_of((1 - tp) * 16, 16), 16)
-    mine = pl.ds(pl.multiple_of(tp * 16, 16), 16)
+                o_all[core, p, rows, :] = own[rows, cols] * spread(f_a, j, p) + from_chip[rows, cols] * spread(f_b, j, p)
+        rows = pl.ds(8 * pieces[i][0], 8 * 8)
+        c = remote(o_all.at[core, :, rows], o_all.at[core, :, rows], o_send.at[i], o_recv.at[i], sibling)
+        c.start()
+        o_copies.append(c)
+
+    low = lax.broadcasted_iota(jnp.int32, (GROUP, 128), 1) < 64
+
+    def fill_lhs(g):
+        rows = pl.ds(pl.multiple_of(g * GROUP, GROUP), GROUP)
+        for p in range(2):
+            for t in range(4):
+                a = o_all[g, p, pl.ds(2 * t, GROUP, stride=8), :]
+                b = o_all[g, p, pl.ds(2 * t + 1, GROUP, stride=8), :]
+                even_k = (2 * p) * 512 + t * 128
+                odd_k = (2 * p + 1) * 512 + t * 128
+                lhs[rows, even_k:even_k + 128] = jnp.where(low, a, pltpu.roll(b, 64, 1)).astype(jnp.bfloat16)
+                lhs[rows, odd_k:odd_k + 128] = jnp.where(low, pltpu.roll(a, 64, 1), b).astype(jnp.bfloat16)
+
+    fill_lhs(core)
+    for c in o_copies:
+        c.wait_recv()
+    fill_lhs(1 - core)
+
+    theirs = pl.ds(pl.multiple_of((1 - tp) * GROUP, GROUP), GROUP)
+    mine = pl.ds(pl.multiple_of(tp * GROUP, GROUP), GROUP)
     tp_copies = []
-    for i, (n, w) in enumerate(n_cols):
+    for i in range(share):
         w_copies[i].wait()
-        y_buf[i, :, 0:w] = lax.dot_general(lhs[...], w_buf[n:n + w, :], (((1,), (1,)), ((), ())), preferred_element_type=jnp.float32)
+        y_buf[i] = lax.dot_general(lhs[...], w_buf[i], (((1,), (1,)), ((), ())), preferred_element_type=jnp.float32)
         c = remote(y_buf.at[i, theirs], from_tp.at[i], tp_send.at[i], tp_recv.at[i], across_y)
         c.start()
         tp_copies.append(c)
 
-    def rows_of(t, q):
-        return pl.ds(pl.multiple_of(q * 32 + t * 16, 16), 16)
-
-    def piece(t, q, half):
-        cols = pl.ds(0, HALF) if half == 0 else pl.ds(HALF, gather.shape[1] - HALF)
-        return gather.at[rows_of(t, q), cols]
-
-    other_sp = lax.rem(sp + 2, 4)
     started = []
 
-    def send(t, q, half, slot, peer):
-        ref = piece(t, q, half)
-        c = remote(ref, ref, ag_send.at[slot, half], ag_recv.at[slot, half], peer)
+    def piece(t, x, block):
+        return gather.at[block, pl.ds(pl.multiple_of(x * 2 * GROUP + t * GROUP, GROUP), GROUP)]
+
+    def send(ref, slot, i, peer):
+        c = remote(ref, ref, ag_send.at[slot, i], ag_recv.at[slot, i], peer)
         c.start()
         started.append(c)
 
-    def arrived(t, q, half, slot):
-        ref = piece(t, q, half)
-        remote(ref, ref, ag_send.at[slot, half], ag_recv.at[slot, half], sibling).wait_recv()
-
-    for half in range(2):
-        for i in range(3 * half, 3 * half + 3):
-            n, w = n_cols[i]
-            tp_copies[i].wait_recv()
-            gather[rows_of(tp, sp), n:n + w] = y_buf[i, mine, 0:w] + from_tp[i, :, 0:w] + bias[0:1, n:n + w]
-        send(tp, sp, half, 0, across_x)
-        send(tp, sp, half, 1, across_y)
-        send(tp, sp, half, 3, sibling)
-    for half in range(2):
-        arrived(tp, other_sp, half, 0)
-        if half == 0:
-            send(tp, other_sp, half, 2, across_y)
-        send(tp, other_sp, half, 4, sibling)
-        arrived(1 - tp, sp, half, 1)
-        if half == 1:
-            send(1 - tp, sp, half, 2, across_x)
-        send(1 - tp, sp, half, 5, sibling)
-    for half in range(2):
-        arrived(1 - tp, other_sp, half, 2)
-        send(1 - tp, other_sp, half, 6, sibling)
-    sib = sp + 1 - 2 * core
-    other_sib = lax.rem(sib + 2, 4)
-    for half in range(2):
-        arrived(tp, sib, half, 3)
-        arrived(tp, other_sib, half, 4)
-        arrived(1 - tp, sib, half, 5)
-        arrived(1 - tp, other_sib, half, 6)
-        lo, hi = (0, HALF) if half == 0 else (HALF, d_out)
-        for n in range(lo, hi, 128):
-            w = min(128, hi - n)
-            y_out[n:n + w, :] = gather[:, n:n + w].T
-    for c in core_copies + chip_copies + tp_copies + started:
+    def arrived(ref, slot, i):
+        remote(ref, ref, ag_send.at[slot, i], ag_recv.at[slot, i], sibling).wait_recv()
+
+    block = [share * core + i for i in range(share)]
+    for i in range(share):
+        tp_copies[i].wait_recv()
+        gather[block[i], pl.ds(pl.multiple_of(chip * 2 * GROUP + tp * GROUP, GROUP), GROUP), :] = y_buf[i, mine] + from_tp[i] + bias[block[i]]
+        ref = piece(tp, chip, block[i])
+        send(ref, 1, i, across_y)
+        send(ref, 0, i, across_x)
+        send(ref, 4, i, sibling)
+    for i in range(share):
+        arrived(piece(1 - tp, chip, block[i]), 1, i)
+        send(piece(1 - tp, chip, block[i]), 2, i, across_x)
+        send(piece(1 - tp, chip, block[i]), 6, i, sibling)
+        arrived(piece(tp, 1 - chip, block[i]), 0, i)
+        send(piece(tp, 1 - chip, block[i]), 5, i, sibling)
+
+    def turn(b):
+        y_out[pl.ds(pl.multiple_of(b * width, width), width), :] = gather[b].T
+
+    for i in range(share):
+        arrived(piece(1 - tp, 1 - chip, block[i]), 2, i)
+        send(piece(1 - tp, 1 - chip, block[i]), 3, i, sibling)
+        turn(block[i])
+    for i in range(share):
+        other = share * (1 - core) + i
+        arrived(piece(tp, chip, other), 4, i)
+        arrived(piece(tp, 1 - chip, other), 5, i)
+        arrived(piece(1 - tp, chip, other), 6, i)
+        arrived(piece(1 - tp, 1 - chip, other), 3, i)
+        turn(other)
+    for c in core_copies + chip_copies + o_copies + tp_copies + started:
         c.wait_send()
 
 
-def exchange(part, q_buf, k_out, v_out, seq_lens, sink_logits, w_o, b_o):
-    d_out = w_o.shape[1]
-    heads = w_o.shape[0]
-    n_col = -(-d_out // COLS)
-    padded = -(-d_out // 128) * 128
+def exchange(part, q_buf, k_out, v_out, seq_lens, sink_logits, w_o, bias):
+    heads, d_out = w_o.shape
+    n_col = bias.shape[0]
+    cols = d_out // n_col
+    share = n_col // 2
     hbm = lambda a: pltpu.with_memory_space_constraint(a, pltpu.HBM)
     vmem = pl.BlockSpec(memory_space=pltpu.VMEM)
     anyw = pl.BlockSpec(memory_space=pltpu.HBM)
@@ -497,29 +510,33 @@
             pltpu.VMEM((2 * GROUP,) + k_out.shape[1:], jnp.bfloat16),
             pltpu.VMEM((2, GROUP * 32, 128), jnp.bfloat16),
             pltpu.VMEM((2,) + block, jnp.float32),
-            pltpu.VMEM((d_out, heads), jnp.bfloat16),
+            pltpu.VMEM((share, cols, heads), jnp.bfloat16),
             pltpu.VMEM((2,) + block, jnp.float32),
             pltpu.VMEM(block, jnp.float32),
             pltpu.VMEM(block, jnp.float32),
             pltpu.VMEM(block, jnp.float32),
-            pltpu.VMEM((2, 256, 128), jnp.float32),
-            pltpu.VMEM((32, heads), jnp.bfloat16),
-            pltpu.VMEM((n_col, 32, COLS), jnp.float32),
-            pltpu.VMEM((n_col, 16, COLS), jnp.float32),
-            pltpu.VMEM((128, padded), jnp.float32),
-            dma((2,)), dma((2, 2)), dma((n_col,)), dma((5,)), dma((5,)), dma((4,)), dma((4,)), dma((n_col,)), dma((n_col,)), dma((7, 2)), dma((7, 2)),
+            pltpu.VMEM((2, 2, 256, 128), jnp.float32),
+            pltpu.VMEM((2 * GROUP, heads), jnp.bfloat16),
+            pltpu.VMEM((share, 2 * GROUP, cols), jnp.float32),
+            pltpu.VMEM((share, GROUP, cols), jnp.float32),
+            pltpu.VMEM((n_col, 128, cols), jnp.float32),
+            dma((2,)), dma((2, 2)), dma((share,)), dma((5,)), dma((5,)), dma((4,)), dma((4,)), dma((4,)), dma((4,)), dma((share,)), dma((share,)),
+            dma((7, share)), dma((7, share)),
         ],
         compiler_params=pltpu.CompilerParams(collective_id=0, has_side_effects=True, vmem_limit_bytes=40 * 1024 * 1024),
         cost_estimate=pl.CostEstimate(flops=4 * 10**8, bytes_accessed=16 * 10**6, transcendentals=10**5),
-      )(part, q_buf, hbm(k_out), hbm(v_out), hbm(seq_lens), hbm(sink_logits), b_o.astype(jnp.float32)[None, :], hbm(w_o.T))
+      )(part, q_buf, hbm(k_out), hbm(v_out), hbm(seq_lens), hbm(sink_logits), bias, hbm(w_o.T))
 
 
 def solution(mesh):
     cache_spec = P("dp", "sp", "tp", None)
 
     def block_step(hidden, seq_lens, rope_cos, rope_sin, k_cache, v_cache, norm_gain, w_qkv, b_qkv, sink_logits, w_o, b_o):
-        k_out, v_out, part, q_buf = local_attention(hidden, seq_lens, rope_cos, rope_sin, k_cache, v_cache, norm_gain, w_qkv, b_qkv, sink_logits)
-        y_t = exchange(part, q_buf, k_out, v_out, seq_lens, sink_logits, w_o, b_o)
+        d_model = hidden.shape[1]
+        gain = norm_gain.astype(jnp.float32).reshape(PARTS, 1, d_model // PARTS)
+        bias = b_o.astype(jnp.float32).reshape(BLOCKS, 1, d_model // BLOCKS)
+        k_out, v_out, part, q_buf = local_attention(hidden, seq_lens, rope_cos, rope_sin, k_cache, v_cache, gain, w_qkv, b_qkv, sink_logits)
+        y_t = exchange(part, q_buf, k_out, v_out, seq_lens, sink_logits, w_o, bias)
         out_hidden = (hidden.T.astype(jnp.float32) + y_t).astype(jnp.bfloat16).T
         seqs, ctx, kv, dim = k_cache.shape
         back = lambda a: a.reshape(seqs, kv, dim, ctx).transpose(0, 3, 1, 2)

time: 55.6 us -> 54.5 us (0.980)
  Pallas kernels: 52 us -> 51.1 us
    reshape x1 -> x2, local copies, waits for them, and re-layouts: 0.78 us -> 1.57 us  [the longest x1 0.78 us: block_step(): bias = b_o.astype(jnp.float32).reshape(BLOCKS, 1, d_model // BLOCKS)]
    broadcast_in_dim x1 -> x0, local copies, waits for them, and re-layouts: 0.7 us -> none  [exchange(): b_o.astype(jnp.float32)[None, :]]
where the time goes in v4:
time: 54.5 us; the launch traced here: 54.4 us
  Pallas kernels  51.1 us (94%)
  local copies, waits for them, and re-layouts  1.57 us (3%)
  other arithmetic  1.01 us (2%)
  between operations  0.66 us (1%)
    pallas_call x1, Pallas kernels, exchange(): pl.pallas_call(exchange_kernel, out_shape=jax.ShapeDtypeStruct((d_out, 12...  29.9 us
    pallas_call x1, Pallas kernels, local_attention(): pl.pallas_call(attend_kernel, out_shape=(jax.ShapeDtypeStruct(k_t.shape,...  21.2 us

profile of v4, /device:TPU:0, one launch (start us, length us, event | category | flops | bytes accessed | tf_op | source)
XLA Modules:
  0.0 54.4 jit_solution(6413013057892486828)
XLA Ops:
  0.6 0.8 %reshape.37.gain_hbm = f32[6,1,480]{2,1,0:T(1,128)S(1)} reshape(bf16[2880]{0:T(1024)(128)(2,1)} %param.18) | data formatting | bytes 17280 | tf_op jit(solution)/shard_map/reshape | solution.py:536
  1.4 0.8 %reshape.39.bias = f32[6,1,480]{2,1,0:T(1,128)S(1)} reshape(bf16[2880]{0:T(1024)(128)(2,1)} %param.23) | data formatting | bytes 17280 | tf_op jit(solution)/shard_map/reshape | solution.py:537
  2.2 21.2 %shard_map.139 = (bf16[128,256,128]{2,1,0:T(8,128)(2,1)}, bf16[128,256,128]{2,1,0:T(8,128)(2,1)}, f32[2,264,256]{2,1,0:T(8,128)S(1)}, f32[2,1088,128]{2,1,0:T(8,128)S(1)}) custom-call(s32[128]{0:T(128)} %lens_hbm.3, f32[32]{0:T(128)} %sinks_hbm.3, bf16[2880,128]{1,0:T(8,128)(2,1)} %bitcast.24, f32[6,1,480]{2,1,0:T(1,128)S(1)} %reshape.37.gain_hbm, ...), custom_call_target="tpu_custom_call" | custom-call | flops 3000000000 | bytes 48000000 | tf_op jit(solution)/shard_map/pallas_call | solution.py:258
  23.4 0.0 copy-start
  23.4 29.9 %shard_map.140 = f32[2880,128]{1,0:T(8,128)S(1)} custom-call(f32[2,264,256]{2,1,0:T(8,128)S(1)} %get-tuple-element.7.part, f32[2,1088,128]{2,1,0:T(8,128)S(1)} %get-tuple-element.8.q_buf, bf16[128,256,128]{2,1,0:T(8,128)(2,1)} %get-tuple-element.9.k_hbm, bf16[128,256,128]{2,1,0:T(8,128)(2,1)} %get-tuple-element.10.v_hbm, s32[128]{0:T(128)} %lens_hbm.3, ...), custom_call_target="tpu_custom_call" | custom-call | flops 400000000 | bytes 16000000 | tf_op jit(solution)/shard_map/pallas_call | solution.py:501
  53.3 0.0 copy-done
  53.4 1.0 %fusion = bf16[128,2880]{0,1:T(8,128)(2,1)} fusion(f32[2880,128]{1,0:T(8,128)S(1)} %shard_map.140, bf16[128,2880]{0,1:T(8,128)(2,1)S(1)} %copy-done), kind=kLoop, calls=%fused_computation.1 | loop fusion | flops 1105920 | bytes 2949120 | tf_op jit(solution)/shard_map/transpose | solution.py:540
Async XLA Ops:
  23.4 29.9 %copy-start = (bf16[128,2880]{0,1:T(8,128)(2,1)S(1)}, bf16[128,2880]{0,1:T(8,128)(2,1)}, u32[]{:S(2)}) copy-start(bf16[128,2880]{0,1:T(8,128)(2,1)} %param.12) | copy-start | bytes 2211844

commit v5 on v4

--- a/solution.py
+++ b/solution.py
@@ -464,10 +464,15 @@
         send(ref, 0, i, across_x)
         send(ref, 4, i, sibling)
     for i in range(share):
-        arrived(piece(1 - tp, chip, block[i]), 1, i)
-        send(piece(1 - tp, chip, block[i]), 2, i, across_x)
+        if i < share - 1:
+            arrived(piece(1 - tp, chip, block[i]), 1, i)
+            send(piece(1 - tp, chip, block[i]), 2, i, across_x)
+            arrived(piece(tp, 1 - chip, block[i]), 0, i)
+        else:
+            arrived(piece(tp, 1 - chip, block[i]), 0, i)
+            send(piece(tp, 1 - chip, block[i]), 2, i, across_y)
+            arrived(piece(1 - tp, chip, block[i]), 1, i)
         send(piece(1 - tp, chip, block[i]), 6, i, sibling)
-        arrived(piece(tp, 1 - chip, block[i]), 0, i)
         send(piece(tp, 1 - chip, block[i]), 5, i, sibling)
 
     def turn(b):

time: 54.5 us -> 53.8 us (0.987)
  Pallas kernels: 51.1 us -> 50.4 us
where the time goes in v5:
time: 53.8 us; the launch traced here: 53.7 us
  Pallas kernels  50.4 us (94%)
  local copies, waits for them, and re-layouts  1.57 us (3%)
  other arithmetic  1.01 us (2%)
  between operations  0.66 us (1%)
    pallas_call x1, Pallas kernels, exchange(): pl.pallas_call(exchange_kernel, out_shape=jax.ShapeDtypeStruct((d_out, 12...  29.4 us
    pallas_call x1, Pallas kernels, local_attention(): pl.pallas_call(attend_kernel, out_shape=(jax.ShapeDtypeStruct(k_t.shape,...  21 us

profile of v5, /device:TPU:0, one launch (start us, length us, event | category | flops | bytes accessed | tf_op | source)
XLA Modules:
  0.0 53.7 jit_solution(17827120183290986297)
XLA Ops:
  0.6 0.8 %reshape.37.gain_hbm = f32[6,1,480]{2,1,0:T(1,128)S(1)} reshape(bf16[2880]{0:T(1024)(128)(2,1)} %param.18) | data formatting | bytes 17280 | tf_op jit(solution)/shard_map/reshape | solution.py:541
  1.4 0.8 %reshape.39.bias = f32[6,1,480]{2,1,0:T(1,128)S(1)} reshape(bf16[2880]{0:T(1024)(128)(2,1)} %param.23) | data formatting | bytes 17280 | tf_op jit(solution)/shard_map/reshape | solution.py:542
  2.2 21.0 %shard_map.139 = (bf16[128,256,128]{2,1,0:T(8,128)(2,1)}, bf16[128,256,128]{2,1,0:T(8,128)(2,1)}, f32[2,264,256]{2,1,0:T(8,128)S(1)}, f32[2,1088,128]{2,1,0:T(8,128)S(1)}) custom-call(s32[128]{0:T(128)} %lens_hbm.3, f32[32]{0:T(128)} %sinks_hbm.3, bf16[2880,128]{1,0:T(8,128)(2,1)} %bitcast.24, f32[6,1,480]{2,1,0:T(1,128)S(1)} %reshape.37.gain_hbm, ...), custom_call_target="tpu_custom_call" | custom-call | flops 3000000000 | bytes 48000000 | tf_op jit(solution)/shard_map/pallas_call | solution.py:258
  23.2 0.0 copy-start
  23.2 29.4 %shard_map.140 = f32[2880,128]{1,0:T(8,128)S(1)} custom-call(f32[2,264,256]{2,1,0:T(8,128)S(1)} %get-tuple-element.7.part, f32[2,1088,128]{2,1,0:T(8,128)S(1)} %get-tuple-element.8.q_buf, bf16[128,256,128]{2,1,0:T(8,128)(2,1)} %get-tuple-element.9.k_hbm, bf16[128,256,128]{2,1,0:T(8,128)(2,1)} %get-tuple-element.10.v_hbm, s32[128]{0:T(128)} %lens_hbm.3, ...), custom_call_target="tpu_custom_call" | custom-call | flops 400000000 | bytes 16000000 | tf_op jit(solution)/shard_map/pallas_call | solution.py:506
  52.6 0.0 copy-done
  52.7 1.0 %fusion = bf16[128,2880]{0,1:T(8,128)(2,1)} fusion(f32[2880,128]{1,0:T(8,128)S(1)} %shard_map.140, bf16[128,2880]{0,1:T(8,128)(2,1)S(1)} %copy-done), kind=kLoop, calls=%fused_computation.1 | loop fusion | flops 1105920 | bytes 2949120 | tf_op jit(solution)/shard_map/transpose | solution.py:545
Async XLA Ops:
  23.2 29.4 %copy-start = (bf16[128,2880]{0,1:T(8,128)(2,1)S(1)}, bf16[128,2880]{0,1:T(8,128)(2,1)}, u32[]{:S(2)}) copy-start(bf16[128,2880]{0,1:T(8,128)(2,1)} %param.12) | copy-start | bytes 2211844
